TPU v7x, 256 devices: a whole 4x4x8 slice. The times are simulated.
256 devices in a mesh: tp: 16 (over z, core), dp: 16 (over x, y).
Axes of the slice: x: 4, y: 4, z: 8, core: 2. Of those that a mesh axis runs over, the one named last changes fastest.
Arguments:
- partials: bfloat16 [16, 512, 16384], P('tp', 'dp'), parts along dimension 1, may hold values from -1.5 to 1.5
- residual: bfloat16 [512, 16384], P('dp'), parts along dimension 0, may hold values from -150 to 150
- gain: bfloat16 [16384], replicated, may hold values from 0.25 to 1.75
- queries: bfloat16 [512, 16384], P('dp', 'tp'), parts along dimension 0, may hold values from -4000 to 4000
- key_cache: bfloat16 [16, 512, 512, 128], P('tp', 'dp'), parts along dimension 1, may hold values from -6 to 6, as said below
- value_cache: bfloat16 [16, 512, 512, 128], P('tp', 'dp'), parts along dimension 1, may hold values from -6 to 6, as said below
- lengths: int32 [512], P('dp'), parts along dimension 0, may hold values from 64 to 512
Outputs:
- new_residual: bfloat16 [512, 16384], P('dp'), parts along dimension 0
- normed: bfloat16 [512, 16384], P('dp'), parts along dimension 0
- token_peak: float32 [512], P('dp'), parts along dimension 0
- attended: bfloat16 [512, 16384], P('dp', 'tp'), parts along dimension 0
There are 16 independent parts, one for each index of `dp`. A program takes and returns all parts, laid end to end along the dimension named above; an argument that names none is the same for every part. Nothing has to cross between parts.
Inputs may be any that keep to these rules, and one draw needn't show every extreme that they name: Slots s and s' of key_cache hold equal keys when s * 8 // 16 == s' * 8 // 16. Slots of value_cache are equal under the same rule as key_cache.
All inputs are finite; a program needn't handle non-finite values.
Results may differ from a plain program's by a relative error of at most 0.0095.
Values may be sent and summed in bfloat16 or wider, within the bound.
No kernel may reach another device: no remote copies, remote signals or barrier semaphores. Data moves between devices by JAX's collectives and lax.ppermute only.
A program may use at most 64 MiB of HBM per device.

v0:
```python
import math

import jax
import jax.numpy as jnp
from jax import lax
from jax.sharding import Mesh
from jax.sharding import PartitionSpec as P

HEAD_DIM = 128
TP = ("tp_0", "tp_1")


def in_blocks(shard, dim, size):
    before, after = (shard.shape[:dim], shard.shape[dim + 1 :])
    return jnp.moveaxis(shard.reshape(*before, size, -1, *after), dim, 0)


def sum_at_owner(shard, axis, dim):
    size = lax.axis_size(axis)
    pieces = lax.all_to_all(in_blocks(shard, dim, size), axis, 0, 0, tiled=True)
    return jnp.sum(pieces.astype(jnp.float32), axis=0)


def summed_rows(shard, axes, dim):
    far, near = axes
    pieces = in_blocks(shard, dim, lax.axis_size(far))
    nearer = sum_at_owner(pieces, near, dim + 1)
    arrived = lax.all_to_all(
        nearer.astype(jnp.bfloat16), far, split_axis=0, concat_axis=0, tiled=True
    )
    return arrived.astype(jnp.float32).sum(axis=0)


def rows_for(lines, size):
    spare = -len(lines) % size
    return jnp.pad(lines, [(0, spare)] + [(0, 0)] * (lines.ndim - 1))


def sent_to_all(shard, axis):
    copies = jnp.broadcast_to(shard, (lax.axis_size(axis), *shard.shape))
    return lax.all_to_all(copies, axis, split_axis=0, concat_axis=0, tiled=True)


def joined_along(pieces, dim):
    lengths = list(pieces.shape[1:])
    lengths[dim] *= pieces.shape[0]
    return jnp.moveaxis(pieces, 0, dim).reshape(lengths)


def gathered_by_axis(shard, axes, dim):
    far, near = axes
    pieces = sent_to_all(sent_to_all(shard, far), near)
    return joined_along(pieces.swapaxes(0, 1).reshape(-1, *shard.shape), dim)


def nested_sum(shard, axes):
    lines = shard.reshape(-1, shard.shape[-1])
    own = summed_rows(rows_for(lines, lax.axis_size(axes[0]) * lax.axis_size(axes[1])), axes, 0)
    whole = gathered_by_axis(own.astype(jnp.bfloat16), axes, 0)
    return whole[: len(lines)].reshape(shard.shape).astype(jnp.float32)


def attend(queries, key_cache, value_cache, lengths):
    seqs = queries.shape[0]
    heads_here = queries.shape[1] // HEAD_DIM
    context = key_cache.shape[2]
    query_blk = queries.reshape(seqs, heads_here, HEAD_DIM)
    scores = jnp.einsum(
        "bhd,bld->bhl", query_blk, key_cache[0], preferred_element_type=jnp.float32
    ) * (1.0 / math.sqrt(HEAD_DIM))
    live = jnp.arange(context, dtype=jnp.int32)[None, :] < lengths[:, None]
    scores = jnp.where(live[:, None, :], scores, -1e30)
    top = jnp.max(scores, axis=2, keepdims=True)
    expo = jnp.exp(scores - top)
    probs = (expo / jnp.sum(expo, axis=2, keepdims=True)).astype(jnp.bfloat16)
    result = jnp.einsum("bhl,bld->bhd", probs, value_cache[0], preferred_element_type=jnp.float32)
    return result.astype(jnp.bfloat16).reshape(seqs, heads_here * HEAD_DIM)


def on_device(partials, residual, gain, queries, key_cache, value_cache, lengths):
    gain_full = gain.astype(jnp.float32)
    terms = partials[0].astype(jnp.float32)
    total = nested_sum(terms.astype(jnp.bfloat16), ("tp_0", "tp_1"))
    hsum = residual.astype(jnp.float32) + total
    inv_rms = lax.rsqrt(jnp.mean(hsum * hsum, axis=1, keepdims=True) + 1e-05)
    scaled = hsum * inv_rms * gain_full[None, :]
    token_peak = jnp.max(jnp.abs(scaled), axis=1)
    new_residual = hsum.astype(jnp.bfloat16)
    normed = scaled.astype(jnp.bfloat16)
    attended = attend(queries, key_cache, value_cache, lengths)
    return (new_residual, normed, token_peak, attended)


def solution(mesh):
    torus = Mesh(mesh.devices.reshape(8, 2, mesh.shape["dp"]), ("tp_0", "tp_1", "dp"))
    return jax.shard_map(
        on_device,
        mesh=torus,
        in_specs=(
            P(TP, "dp", None),
            P("dp", None),
            P(),
            P("dp", TP),
            P(TP, "dp", None, None),
            P(TP, "dp", None, None),
            P("dp"),
        ),
        out_specs=(P("dp", None), P("dp", None), P("dp"), P("dp", TP)),
        check_vma=False,
    )
```

profile of v0, /device:TPU:1, one launch (start us, length us, event | category | flops | bytes accessed | tf_op | source)
XLA Modules:
  0.0 72.5 jit_solution(3234575777562936657)
XLA Ops:
  0.6 1.7 %reshape_reshape.4 = bf16[8,2,2,16384]{3,2,1,0:T(2,128)(2,1)S(1)} reshape(bf16[1,32,16384]{2,1,0:T(8,128)(2,1)} %param.7) | data formatting | bytes 2097152 | tf_op jit(solution)/shard_map/reshape;reshape | solution.py:15
  2.4 0.8 %copy.15 = bf16[2,8,2,16384]{3,2,1,0:T(2,128)(2,1)S(1)} copy(bf16[2,8,2,16384]{3,2,0,1:T(2,128)(2,1)S(1)} %bitcast.24) | data formatting | bytes 2097152 | tf_op jit(solution)/shard_map/transpose | solution.py:15
  3.2 7.4 %all_to_all.20 = bf16[2,8,2,16384]{3,2,1,0:T(2,128)(2,1)S(1)} all-to-all(bf16[2,8,2,16384]{3,2,1,0:T(2,128)(2,1)S(1)} %copy.15), channel_id=1, replica_groups=mesh['tp_0'=8,'tp_1'=2,'dp'=16] {'tp_1'}, dimensions={0} | all-to-all | bytes 2097152 | tf_op jit(solution)/shard_map/all_to_all | solution.py:20
  10.6 2.5 %reduce_sum.42 = bf16[8,2,16384]{2,1,0:T(2,128)(2,1)S(1)} reduce(bf16[2,8,2,16384]{3,2,1,0:T(2,128)(2,1)S(1)} %all_to_all.20, bf16[]{:T(256)} %constant.3.clone.1), dimensions={0}, to_apply=%region_0.1 | reduce | flops 262144 | bytes 1572866 | tf_op jit(solution)/shard_map/reduce_sum | solution.py:21
  13.1 23.0 %all_to_all.21 = bf16[8,2,16384]{2,1,0:T(2,128)(2,1)S(1)} all-to-all(bf16[8,2,16384]{2,1,0:T(2,128)(2,1)S(1)} %reduce_sum.42), channel_id=1, replica_groups=mesh['tp_0'=8,'tp_1'=2,'dp'=16] {'tp_0'}, dimensions={0} | all-to-all | bytes 1048576 | tf_op jit(solution)/shard_map/all_to_all | solution.py:28
  36.1 0.5 reduce_sum.43
  36.6 1.1 %broadcast_in_dim.16 = bf16[8,2,16384]{2,1,0:T(2,128)(2,1)} broadcast(bf16[2,16384]{1,0:T(2,128)(2,1)S(1)} %reduce_sum.43), dimensions={1,2} | broadcast | bytes 589824 | tf_op jit(solution)/shard_map/broadcast_in_dim | solution.py:40
  37.7 3.5 %all-to-all-start.2 = ((bf16[8,2,16384]{2,1,0:T(2,128)(2,1)}), bf16[8,2,16384]{2,1,0:T(2,128)(2,1)S(1)}, u32[]{:S(2)}, u32[]{:S(2)}) async-start(bf16[8,2,16384]{2,1,0:T(2,128)(2,1)} %broadcast_in_dim.16), calls=%async_computation.2 | async-start | bytes 1048576 | tf_op jit(solution)/shard_map/all_to_all | solution.py:41
  41.2 0.0 copy-done.3
  41.2 0.1 iota_compare_fusion
  41.3 0.0 copy-done.2
  41.3 0.0 copy-done.1
  41.3 3.4 %fusion.11 = f32[32,8,512]{2,1,0:T(8,128)S(1)} fusion(bf16[32,8,128]{2,1,0:T(8,128)(2,1)S(1)} %bitcast.26, bf16[1,32,512,128]{3,2,1,0:T(8,128)(2,1)} %param.11, pred[32,512]{1,0:T(8,128)(4,1)S(1)} %iota_compare_fusion), kind=kOutput, calls=%fused_computation.14 | convolution fusion | flops 33816576 | bytes 4800512 | tf_op jit(solution)/shard_map/bhd,bld->bhl/dot_general | solution.py:68
  44.7 0.2 fusion.19
  45.0 2.9 %fusion.14 = bf16[32,8,128]{2,1,0:T(8,128)(2,1)S(1)} fusion(bf16[1,32,512,128]{3,2,1,0:T(8,128)(2,1)} %param.12, f32[32,8]{1,0:T(8,128)S(1)} %fusion.19, f32[32,8,512]{2,1,0:T(8,128)S(1)} %fusion.11), kind=kOutput, calls=%fused_computation.15 | convolution fusion | flops 33981184 | bytes 4785152 | tf_op jit(solution)/shard_map/bhl,bld->bhd/dot_general | solution.py:76
  47.9 0.7 copy.22
  48.5 8.6 %all-to-all-done.2 = bf16[8,2,16384]{2,1,0:T(2,128)(2,1)S(1)} async-done(((bf16[8,2,16384]{2,1,0:T(2,128)(2,1)}), bf16[8,2,16384]{2,1,0:T(2,128)(2,1)S(1)}, u32[]{:S(2)}, u32[]{:S(2)}) %all-to-all-start.2) | async-done | bytes 524320 | tf_op jit(solution)/shard_map/all_to_all | solution.py:41
  57.1 0.8 %broadcast_in_dim.26 = bf16[2,8,2,16384]{3,2,1,0:T(2,128)(2,1)S(1)} broadcast(bf16[8,2,16384]{2,1,0:T(2,128)(2,1)S(1)} %all-to-all-done.2), dimensions={1,2,3} | broadcast | bytes 1572864 | tf_op jit(solution)/shard_map/broadcast_in_dim | solution.py:40
  57.9 6.6 %all_to_all.22 = bf16[2,8,2,16384]{3,2,1,0:T(2,128)(2,1)S(1)} all-to-all(bf16[2,8,2,16384]{3,2,1,0:T(2,128)(2,1)S(1)} %broadcast_in_dim.26), channel_id=1, replica_groups=mesh['tp_0'=8,'tp_1'=2,'dp'=16] {'tp_1'}, dimensions={0} | all-to-all | bytes 2097152 | tf_op jit(solution)/shard_map/all_to_all | solution.py:41
  64.6 0.9 %convert_bitcast_fusion = f32[8,2,2,16384]{3,2,0,1:T(2,128)S(1)} fusion(bf16[2,8,2,16384]{3,2,1,0:T(2,128)(2,1)S(1)} %all_to_all.22), kind=kLoop, calls=%fused_computation.5 | loop fusion | flops 524288 | bytes 3145728 | tf_op jit(solution)/shard_map/convert_element_type | solution.py:60
  65.5 1.5 %copy.17 = f32[8,2,2,16384]{3,2,1,0:T(2,128)} copy(f32[8,2,2,16384]{3,2,0,1:T(2,128)S(1)} %convert_bitcast_fusion) | data formatting | bytes 4194304 | tf_op jit(solution)/shard_map/convert_element_type | solution.py:60
  67.0 2.8 %reshape.47 = f32[32,16384]{1,0:T(8,128)S(1)} reshape(f32[8,2,2,16384]{3,2,1,0:T(2,128)} %copy.17) | data formatting | bytes 4194304 | tf_op jit(solution)/shard_map/convert_element_type | solution.py:60
  69.7 0.4 multiply_reduce_fusion
  70.1 2.3 %abs_reduce_fusion = (f32[32]{0:T(128)}, bf16[32,16384]{1,0:T(8,128)(2,1)}, bf16[32,16384]{1,0:T(8,128)(2,1)}) fusion(f32[16384]{0:T(1024)S(1)} %convert_element_type.38, f32[32]{0:T(128)S(1)} %add_rsqrt_fusion, f32[32,16384]{1,0:T(8,128)S(1)} %reshape.47, bf16[32,16384]{1,0:T(8,128)(2,1)S(1)} %copy-done), kind=kLoop, calls=%fused_computation.6 | loop fusion | flops 4194272 | bytes 5308672 | tf_op jit(solution)/shard_map/reduce_max | solution.py:87
  (8 shorter events, 0.0 us)
Async XLA Ops:
  10.6 30.6 %copy-start.3 = (s32[32]{0:T(128)S(1)}, s32[32]{0:T(128)}, u32[]{:S(2)}) copy-start(s32[32]{0:T(128)} %param.13) | copy-start | bytes 388
  10.6 30.7 %copy-start.2 = (bf16[16384]{0:T(1024)(128)(2,1)S(1)}, bf16[16384]{0:T(1024)(128)(2,1)}, u32[]{:S(2)}) copy-start(bf16[16384]{0:T(1024)(128)(2,1)} %param.9) | copy-start | bytes 98308
  10.6 30.8 %copy-start.1 = (bf16[32,1024]{1,0:T(8,128)(2,1)S(1)}, bf16[32,1024]{1,0:T(8,128)(2,1)}, u32[]{:S(2)}) copy-start(bf16[32,1024]{1,0:T(8,128)(2,1)} %param.10) | copy-start | bytes 196612
  37.7 19.4 %all-to-all-start.2 = ((bf16[8,2,16384]{2,1,0:T(2,128)(2,1)}), bf16[8,2,16384]{2,1,0:T(2,128)(2,1)S(1)}, u32[]{:S(2)}, u32[]{:S(2)}) async-start(bf16[8,2,16384]{2,1,0:T(2,128)(2,1)} %broadcast_in_dim.16), calls=%async_computation.2 | async-start | bytes 1048576 | tf_op jit(solution)/shard_map/all_to_all | solution.py:41
  66.9 2.8 %copy-start = (bf16[32,16384]{1,0:T(8,128)(2,1)S(1)}, bf16[32,16384]{1,0:T(8,128)(2,1)}, u32[]{:S(2)}) copy-start(bf16[32,16384]{1,0:T(8,128)(2,1)} %param.8) | copy-start | bytes 3145732
where the time goes:
time: 72.8 us; the launch traced here: 72.5 us
  blocking collectives  37 us (51%)
  local copies, waits for them, and re-layouts  9.34 us (13%)
  waiting for transfers between devices  8.59 us (12%)
  other arithmetic  6.98 us (10%)
  matrix products  6.28 us (9%)
  starting transfers between devices  3.49 us (5%)
  between operations  0.75 us (1%)
    all_to_all x1, blocking collectives, summed_rows(): lax.all_to_all(nearer.astype(jnp.bfloat16), far, split_axis=0, concat_axi...  23 us
    all_to_all x1, waiting for transfers between devices, sent_to_all(): return lax.all_to_all(copies, axis, split_axis=0, concat_axis=0, tiled=True)  8.59 us
    all_to_all x1, blocking collectives, sum_at_owner(): pieces = lax.all_to_all(in_blocks(shard, dim, size), axis, 0, 0, tiled=True)  7.4 us
    all_to_all x1, blocking collectives, sent_to_all(): return lax.all_to_all(copies, axis, split_axis=0, concat_axis=0, tiled=True)  6.64 us
    convert_element_type x2, local copies, waits for them, and re-layouts, nested_sum(): return whole[:len(lines)].reshape(shard.shape).astype(jnp.float32)  4.28 us
    all_to_all x1, starting transfers between devices, sent_to_all(): return lax.all_to_all(copies, axis, split_axis=0, concat_axis=0, tiled=True)  3.49 us
    dot_general x1, matrix products, attend(): jnp.einsum('bhd,bld->bhl', query_blk, key_cache[0], preferred_element_typ...  3.38 us
    dot_general x1, matrix products, attend(): jnp.einsum('bhl,bld->bhd', probs, value_cache[0], preferred_element_type=...  2.9 us
  transfers between devices with their start and end apart: 1, of which 1 were waited for; matrix products, arithmetic and copies ran while one was open for 10% of the time, Pallas kernels for 0%

commit v1 on v0

v1 whole, which is shorter than its diff:
```python
import functools
import math

import jax
import jax.numpy as jnp
from jax import lax
from jax.experimental import pallas as pl
from jax.experimental.pallas import tpu as pltpu
from jax.sharding import PartitionSpec as P


HEAD_DIM = 128
CHIPS = 8
CHUNK = 2048
HALF = 1024
SEQ_GROUPS = 2

f32, bf16 = jnp.float32, jnp.bfloat16
ANY = pl.BlockSpec(memory_space=pl.ANY)
VMEM = pl.BlockSpec(memory_space=pltpu.VMEM)
SMALL = pltpu.CompilerParams(vmem_limit_bytes=16 << 20)


def near(x):
    return pltpu.with_memory_space_constraint(x, pltpu.VMEM)


def far(x):
    return pltpu.with_memory_space_constraint(x, pltpu.HBM)


def onchip(shape, dtype):
    return pltpu.VMEM(shape, dtype)


def place():
    me = lax.axis_index("tp")
    core = lax.rem(me, 2)
    return me // 2, core, 1 - 2 * core


def chunk_at(chip, steps):
    return lax.rem(chip + steps + 2 * CHIPS, CHIPS)


def columns(start, size):
    return pl.ds(pl.multiple_of(start, HALF), size)


def cost(flops, nbytes):
    return pl.CostEstimate(flops=flops, bytes_accessed=nbytes, transcendentals=0)


def along(x, hops):
    pairs = []
    for chip in range(CHIPS):
        pairs.append((2 * chip, 2 * ((chip + hops) % CHIPS)))
        pairs.append((2 * chip + 1, 2 * ((chip - hops) % CHIPS) + 1))
    return lax.ppermute(x, "tp", pairs)


def across(x):
    return lax.ppermute(x, "tp", [(i, i ^ 1) for i in range(2 * CHIPS)])


def handled(chip, core, way):
    return [
        (chunk_at(chip, 4) * CHUNK + core * HALF, HALF),
        (chunk_at(chip, 3 * way) * CHUNK, CHUNK),
        (chunk_at(chip, way) * CHUNK, CHUNK),
        (chunk_at(chip, 2 * way) * CHUNK, CHUNK),
        (chip * CHUNK + core * HALF, HALF),
    ]


def copy_ranges(src, dst, ranges, sems):
    copies, at = [], 0
    for i, (start, size) in enumerate(ranges):
        copies.append(
            pltpu.make_async_copy(
                src.at[:, columns(start, size)], dst.at[:, pl.ds(at, size)], sems.at[i]
            )
        )
        at += size
    return copies


def pack_kernel(p_ref, send_ref, sems):
    chip, core, way = place()
    copies = copy_ranges(p_ref, send_ref, handled(chip, 1 - core, -way), sems)
    for c in copies:
        c.start()
    for c in copies:
        c.wait()


def keep_kernel(p_ref, r_ref, keep_ref, res_ref, sems):
    chip, core, way = place()
    copies = copy_ranges(p_ref, keep_ref, handled(chip, core, way), sems)
    copies.append(
        pltpu.make_async_copy(r_ref.at[:, columns(chip * CHUNK, CHUNK)], res_ref, sems.at[5])
    )
    for c in copies:
        c.start()
    for c in copies:
        c.wait()


def presum_kernel(keep_ref, got_ref, a4_ref, a3_ref, a1_ref, s2_ref, s0_ref):
    at = 0
    for out in (a4_ref, a3_ref, a1_ref, s2_ref, s0_ref):
        size = out.shape[1]
        mine = keep_ref[:, at : at + size].astype(f32)
        out[...] = (mine + got_ref[:, at : at + size].astype(f32)).astype(bf16)
        at += size


def relay_kernel(s2_ref, r3_ref, r4_ref, m_ref):
    _, core, _ = place()
    for half in range(2):
        cols = slice(half * HALF, (half + 1) * HALF)
        both = s2_ref[:, cols].astype(f32) + r3_ref[:, cols].astype(f32)
        here = jnp.where(core == half, 1.0, 0.0).astype(f32)
        m_ref[:, cols] = (both + here * r4_ref[...].astype(f32)).astype(bf16)


def arrive_kernel(r1_ref, rm_ref, s0_ref, t_ref):
    _, core, _ = place()
    for half in range(2):
        cols = slice(half * HALF, (half + 1) * HALF)
        both = r1_ref[:, cols].astype(f32) + rm_ref[:, cols].astype(f32)
        here = jnp.where(core == half, 1.0, 0.0).astype(f32)
        t_ref[:, cols] = (both + here * s0_ref[...].astype(f32)).astype(bf16)


def hsum_kernel(t_ref, rt_ref, res_ref, n_ref):
    total = t_ref[...].astype(f32) + rt_ref[...].astype(f32)
    n_ref[...] = (res_ref[...].astype(f32) + total).astype(bf16)


def fork_kernel(g1_ref, g2_ref, half_ref, both_ref):
    _, core, _ = place()
    half_ref[...] = g2_ref[:, columns(core * HALF, HALF)]
    both_ref[:, :CHUNK] = g1_ref[...]
    both_ref[:, CHUNK:] = g2_ref[...]


def pieces(chip, core, way, n, g1, g2, w12, g3=None, g4=None, w34=None):
    across_ring = chunk_at(chip, 4) * 2
    early = [
        (n, 0, 2 * chip, 2),
        (g1, 0, 2 * chunk_at(chip, -way), 2),
        (g2, 0, 2 * chunk_at(chip, -2 * way), 2),
        (w12, 0, 2 * chunk_at(chip, way), 2),
        (w12, CHUNK, 2 * chunk_at(chip, 2 * way), 2),
    ]
    late = [
        (g3, 0, 2 * chunk_at(chip, -3 * way), 2),
        (g4, 0, across_ring + core, 1),
        (w34, 0, 2 * chunk_at(chip, 3 * way), 2),
        (w34, CHUNK, across_ring + 1 - core, 1),
    ]
    return early, late


def by_half(wide):
    return [(ref, at + k * HALF, block + k) for ref, at, block, n in wide for k in range(n)]


def write_out(wide, out, sems):
    copies = []
    for i, (ref, at, block, n) in enumerate(wide):
        copies.append(
            pltpu.make_async_copy(
                ref.at[:, pl.ds(at, n * HALF)], out.at[:, columns(block * HALF, n * HALF)], sems.at[i]
            )
        )
        copies[-1].start()
    return copies


def add_squares(wide, sq_ref):
    for ref, at, block in by_half(wide):
        part = jnp.zeros(sq_ref.shape[1:], f32)
        for j in range(0, HALF, 128):
            x = ref[:, at + j : at + j + 128].astype(f32)
            part += x * x
        sq_ref[block] = part


def early_kernel(n_ref, g1_ref, g2_ref, w12_ref, res_out, sq_ref, sems):
    early, _ = pieces(*place(), n_ref, g1_ref, g2_ref, w12_ref)
    copies = write_out(early, res_out, sems)
    sq_ref[...] = jnp.zeros_like(sq_ref)
    add_squares(early, sq_ref)
    for copy in copies:
        copy.wait()


def finish_kernel(
    n_ref, g1_ref, g2_ref, w12_ref, g3_ref, g4_ref, w34_ref, gain_ref, early_sq, _,
    res_out, norm_out, peak_ref, y_ref, sq_ref, res_sems, norm_sems,
):
    early, late = pieces(
        *place(), n_ref, g1_ref, g2_ref, w12_ref, g3_ref, g4_ref, w34_ref
    )
    tokens, features = res_out.shape
    copies = write_out(late, res_out, res_sems)
    sq_ref[...] = early_sq[...]
    add_squares(late, sq_ref)
    total = sq_ref[0]
    for block in range(1, features // HALF):
        total += sq_ref[block]
    mean = jnp.sum(total, axis=1, keepdims=True) * (1.0 / features)
    inv = jnp.broadcast_to(lax.rsqrt(mean + 1e-05), (tokens, 128))
    peak = jnp.zeros((tokens, 128), f32)
    for i, (ref, at, block) in enumerate(by_half(early + late)):
        gains = gain_ref[block]
        for j in range(0, HALF, 128):
            x = ref[:, at + j : at + j + 128].astype(f32)
            y = x * inv * gains[:, j : j + 128]
            peak = jnp.maximum(peak, jnp.abs(y))
            y_ref[:, i * HALF + j : i * HALF + j + 128] = y.astype(bf16)
        copies.append(
            pltpu.make_async_copy(
                y_ref.at[:, pl.ds(i * HALF, HALF)],
                norm_out.at[:, columns(block * HALF, HALF)],
                norm_sems.at[i],
            )
        )
        copies[-1].start()
    peak_ref[...] = jnp.max(peak.T, axis=0, keepdims=True)
    for copy in copies:
        copy.wait()


def attend_kernel(first, q_ref, k_ref, v_ref, len_ref, *refs):
    o_ref, q_rows, o_rows, stage, values, sem, v_sems = refs[-7:]
    seqs, width = stage.shape
    heads = width // HEAD_DIM
    rows = seqs * heads
    context = k_ref.shape[1]
    mine = slice(first, first + seqs)
    fetched = [
        pltpu.make_async_copy(v_ref.at[first + i], values.at[i], v_sems.at[i]) for i in range(seqs)
    ]
    for copy in fetched:
        copy.start()
    for h in range(heads):
        cols = slice(h * HEAD_DIM, (h + 1) * HEAD_DIM)
        q_rows[pl.ds(h, seqs, stride=heads), :] = q_ref[mine, cols].astype(f32)
    turned = q_rows[...].T
    owner = lax.broadcasted_iota(jnp.int32, (HEAD_DIM, rows), 1) // heads
    scores = jnp.zeros((context, rows), f32)
    for i in range(seqs):
        own = jnp.where(owner == i, turned, 0.0).astype(bf16)
        scores += jnp.dot(k_ref[first + i], own, preferred_element_type=f32)
    lens = len_ref[mine, :]
    spread = lax.broadcasted_iota(jnp.int32, (seqs, rows), 0)
    spread = spread == lax.broadcasted_iota(jnp.int32, (seqs, rows), 1) // heads
    lens = jnp.sum(jnp.where(spread, lens, 0), axis=0, keepdims=True)
    live = lax.broadcasted_iota(jnp.int32, (context, rows), 0) < lens
    scores = jnp.where(live, scores * (1.0 / math.sqrt(HEAD_DIM)), -1e30)
    expo = jnp.exp(scores - jnp.max(scores, axis=0, keepdims=True))
    probs = (expo * (1.0 / jnp.sum(expo, axis=0, keepdims=True))).T
    for i in range(seqs):
        fetched[i].wait()
        o_rows[i * heads : (i + 1) * heads, :] = jnp.dot(
            probs[i * heads : (i + 1) * heads, :].astype(bf16),
            values[i],
            preferred_element_type=f32,
        )
    for h in range(heads):
        stage[:, h * HEAD_DIM : (h + 1) * HEAD_DIM] = o_rows[
            pl.ds(h, seqs, stride=heads), :
        ].astype(bf16)
    copy = pltpu.make_async_copy(stage, o_ref.at[mine, :], sem)
    copy.start()
    copy.wait()


def attend(queries, keys, values, lens):
    seqs, width = queries.shape
    rows = seqs // SEQ_GROUPS * (width // HEAD_DIM)
    nbytes = 4 * keys.size // SEQ_GROUPS
    out = []
    for g in range(SEQ_GROUPS):
        out = [
            pl.pallas_call(
                functools.partial(attend_kernel, g * (seqs // SEQ_GROUPS)),
                out_shape=jax.ShapeDtypeStruct((seqs, width), bf16),
                in_specs=[VMEM, VMEM, ANY, VMEM] + [ANY] * len(out),
                out_specs=ANY,
                scratch_shapes=[
                    pltpu.VMEM((rows, HEAD_DIM), f32),
                    pltpu.VMEM((rows, HEAD_DIM), f32),
                    pltpu.VMEM((seqs // SEQ_GROUPS, width), bf16),
                    pltpu.VMEM((seqs // SEQ_GROUPS, *values.shape[1:]), bf16),
                    pltpu.SemaphoreType.DMA,
                    pltpu.SemaphoreType.DMA((seqs // SEQ_GROUPS,)),
                ],
                input_output_aliases={4: 0} if out else {},
                cost_estimate=cost(200_000_000, nbytes),
                compiler_params=SMALL,
            )(queries, keys, far(values), near(lens), *out)
        ]
    return out[0]


def summed_and_normed(partial, residual, gain):
    tokens, features = partial.shape
    dma = pltpu.SemaphoreType.DMA

    def held(width):
        return onchip((tokens, width), bf16)

    def call(kernel, outs, *args, in_specs=None, scratch=(), flops=1000):
        args = [far(a) if in_specs else near(a) for a in args]
        return pl.pallas_call(
            kernel,
            out_shape=outs,
            in_specs=in_specs or [VMEM] * len(args),
            out_specs=jax.tree.map(lambda _: VMEM, outs),
            scratch_shapes=list(scratch),
            cost_estimate=cost(flops, 1 << 20),
            compiler_params=SMALL,
        )(*args)

    send = call(pack_kernel, held(8192), partial, in_specs=[ANY], scratch=[dma((5,))])
    got = across(send)
    keep, res = call(
        keep_kernel, (held(8192), held(CHUNK)), partial, residual,
        in_specs=[ANY, ANY], scratch=[dma((6,))],
    )
    a4, a3, a1, s2, s0 = call(
        presum_kernel, (held(HALF), held(CHUNK), held(CHUNK), held(CHUNK), held(HALF)), keep, got
    )
    r4 = along(a4, 2)
    r3 = along(a3, 1)
    r1 = along(a1, 1)
    m = call(relay_kernel, held(CHUNK), s2, r3, r4)
    rm = along(m, 2)
    t = call(arrive_kernel, held(CHUNK), r1, rm, s0)
    rt = across(t)
    n = call(hsum_kernel, held(CHUNK), t, rt, res)
    g2 = along(n, 2)
    g1 = along(n, 1)
    half, both = call(fork_kernel, (held(HALF), held(2 * CHUNK)), g1, g2)
    g3 = along(g2, 1)
    g4 = along(half, 2)
    w12 = across(both)
    last = jnp.concatenate([g3, g4], axis=1)
    w34 = across(last)
    blocks = features // HALF
    gains = gain.astype(f32).reshape(blocks, 1, HALF)
    whole = jax.ShapeDtypeStruct((tokens, features), bf16)
    begun, squares = pl.pallas_call(
        early_kernel,
        out_shape=(whole, onchip((blocks, tokens, 128), f32)),
        in_specs=[VMEM] * 4,
        out_specs=(ANY, VMEM),
        scratch_shapes=[dma((5,))],
        cost_estimate=cost(1_000_000, 1 << 20),
        compiler_params=SMALL,
        name="early",
    )(*map(near, (n, g1, g2, w12)))
    res_out, norm_out, peak = pl.pallas_call(
        finish_kernel,
        out_shape=(whole, whole, jax.ShapeDtypeStruct((1, tokens), f32)),
        in_specs=[VMEM] * 9 + [ANY],
        out_specs=(ANY, ANY, VMEM),
        scratch_shapes=[
            pltpu.VMEM((tokens, features), bf16),
            pltpu.VMEM((blocks, tokens, 128), f32),
            dma((4,)),
            dma((blocks,)),
        ],
        input_output_aliases={9: 0},
        cost_estimate=cost(1_000_000, 4 << 20),
        compiler_params=SMALL,
        name="finish",
    )(*map(near, (n, g1, g2, w12, g3, g4, w34, gains, squares)), begun)
    return res_out, norm_out, peak.reshape(tokens)


def on_device(partials, residual, gain, queries, key_cache, value_cache, lengths):
    lens = jnp.broadcast_to(lengths[:, None], (lengths.shape[0], 128))
    attended = attend(queries, key_cache[0], value_cache[0], lens)
    new_residual, normed, token_peak = summed_and_normed(partials[0], residual, gain)
    return (new_residual, normed, token_peak, attended)


def solution(mesh):
    return jax.shard_map(
        on_device,
        mesh=mesh,
        in_specs=(
            P("tp", "dp", None),
            P("dp", None),
            P(),
            P("dp", "tp"),
            P("tp", "dp", None, None),
            P("tp", "dp", None, None),
            P("dp"),
        ),
        out_specs=(P("dp", None), P("dp", None), P("dp"), P("dp", "tp")),
        check_vma=False,
    )
```

time: 72.8 us -> 54.5 us (0.75)
  blocking collectives: 37 us -> 0 us
  starting transfers between devices: 3.49 us -> 25.7 us
  Pallas kernels: 0 us -> 15.2 us
  local copies, waits for them, and re-layouts: 9.34 us -> 0.09 us
  other arithmetic: 6.98 us -> 0.02 us
  matrix products: 6.28 us -> 0 us
  waiting for transfers between devices: 8.59 us -> 12.6 us
    all_to_all x3 -> x0, blocking collectives: 37 us -> none  [the longest x1 23 us: summed_rows(): lax.all_to_all(nearer.astype(jnp.bfloat16), far, split_axis=0, concat_axi...]
    ppermute x0 -> x12, starting transfers between devices: none -> 25.7 us  [the longest x8 14.8 us: along(): return lax.ppermute(x, 'tp', pairs)]
    pallas_call x0 -> x11, Pallas kernels: none -> 15.2 us  [the longest x2 9.48 us: attend(): pl.pallas_call(functools.partial(attend_kernel, g * (seqs // SEQ_GROUPS))...]
    ppermute x0 -> x12, waiting for transfers between devices: none -> 12.6 us  [the longest x8 11.3 us: along(): return lax.ppermute(x, 'tp', pairs)]
    all_to_all x1 -> x0, waiting for transfers between devices: 8.59 us -> none  [sent_to_all(): return lax.all_to_all(copies, axis, split_axis=0, concat_axis=0, tiled=True)]
    dot_general x2 -> x0, matrix products: 6.28 us -> none  [the longest x1 3.38 us: attend(): jnp.einsum('bhd,bld->bhl', query_blk, key_cache[0], preferred_element_typ...]
    convert_element_type x2 -> x0, local copies, waits for them, and re-layouts: 4.28 us -> none  [nested_sum(): return whole[:len(lines)].reshape(shard.shape).astype(jnp.float32)]
    all_to_all x1 -> x0, starting transfers between devices: 3.49 us -> none  [sent_to_all(): return lax.all_to_all(copies, axis, split_axis=0, concat_axis=0, tiled=True)]
  transfers between devices with their start and end apart: 1 -> 12, of which waited for: 1 -> 6; matrix products, arithmetic and copies ran while one was open for 10% -> 0% of each run, Pallas kernels for 0% -> 21%
where the time goes in v1:
time: 54.5 us; the launch traced here: 54.4 us
  starting transfers between devices  25.7 us (47%)
  Pallas kernels  15.2 us (28%)
  waiting for transfers between devices  12.6 us (23%)
  between operations  0.77 us (1%)
    ppermute x8, starting transfers between devices, along(): return lax.ppermute(x, 'tp', pairs)  14.8 us
    ppermute x8, waiting for transfers between devices, along(): return lax.ppermute(x, 'tp', pairs)  11.3 us
    ppermute x4, starting transfers between devices, across(): return lax.ppermute(x, 'tp', [(i, i ^ 1) for i in range(2 * CHIPS)])  10.9 us
    pallas_call x2, Pallas kernels, attend(): pl.pallas_call(functools.partial(attend_kernel, g * (seqs // SEQ_GROUPS))...  9.48 us
    pallas_call x7, Pallas kernels, call(): pl.pallas_call(kernel, out_shape=outs, in_specs=in_specs or [VMEM] * len(...  2.81 us
    pallas_call x1, Pallas kernels, summed_and_normed(): pl.pallas_call(finish_kernel, out_shape=(whole, whole, jax.ShapeDtypeStru...  2.05 us
    ppermute x4, waiting for transfers between devices, across(): return lax.ppermute(x, 'tp', [(i, i ^ 1) for i in range(2 * CHIPS)])  1.3 us
  transfers between devices with their start and end apart: 12, of which 6 were waited for; matrix products, arithmetic and copies ran while one was open for 0% of the time, Pallas kernels for 21%

profile of v1, /device:TPU:1, one launch (start us, length us, event | category | flops | bytes accessed | tf_op | source)
XLA Modules:
  0.0 54.4 jit_solution(6945498048216699328)
XLA Ops:
  0.7 1.3 %shard_map.103 = bf16[32,8192]{1,0:T(8,128)(2,1)S(1)} custom-call(bf16[32,16384]{1,0:T(8,128)(2,1)} %bitcast.10), custom_call_target="tpu_custom_call" | custom-call | flops 1000 | bytes 1048576 | tf_op jit(solution)/shard_map/pallas_call | solution.py:319
  2.0 3.3 %collective-permute-start = (bf16[32,8192]{1,0:T(8,128)(2,1)S(1)}, bf16[32,8192]{1,0:T(8,128)(2,1)S(1)}, u32[]{:S(2)}, u32[]{:S(2)}) collective-permute-start(bf16[32,8192]{1,0:T(8,128)(2,1)S(1)} %shard_map.103), channel_id=1, source_target_pairs={{0,16},{16,0},{32,48},{48,32},{64,80},{80,64},{96,112},{112,96},{1... | collective-permute-start | bytes 1572872 | tf_op jit(solution)/shard_map/ppermute | solution.py:63
  5.2 1.2 %shard_map.102 = (bf16[32,8192]{1,0:T(8,128)(2,1)S(1)}, bf16[32,2048]{1,0:T(8,128)(2,1)S(1)}) custom-call(bf16[32,16384]{1,0:T(8,128)(2,1)} %bitcast.11, bf16[32,16384]{1,0:T(8,128)(2,1)} %r_ref.1), custom_call_target="tpu_custom_call" | custom-call | flops 1000 | bytes 1048576 | tf_op jit(solution)/shard_map/pallas_call | solution.py:319
  6.5 0.3 collective-permute-done.got_ref
  6.8 0.1 shard_map.104
  6.9 3.9 %collective-permute-start.2 = (bf16[32,2048]{1,0:T(8,128)(2,1)S(1)}, bf16[32,2048]{1,0:T(8,128)(2,1)S(1)}, u32[]{:S(2)}, u32[]{:S(2)}) collective-permute-start(bf16[32,2048]{1,0:T(8,128)(2,1)S(1)} %get-tuple-element.21), channel_id=1, source_target_pairs={{0,32},{16,240},{32,64},{48,16},{64,96},{80,48},{96,128},{112,80},... | collective-permute-start | bytes 393224 | tf_op jit(solution)/shard_map/ppermute | solution.py:59
  10.9 1.2 %collective-permute-start.3 = (bf16[32,1024]{1,0:T(8,128)(2,1)S(1)}, bf16[32,1024]{1,0:T(8,128)(2,1)S(1)}, u32[]{:S(2)}, u32[]{:S(2)}) collective-permute-start(bf16[32,1024]{1,0:T(8,128)(2,1)S(1)} %get-tuple-element.22), channel_id=1, source_target_pairs={{0,64},{16,208},{32,96},{48,240},{64,128},{80,16},{96,160},{112,48... | collective-permute-start | bytes 196616 | tf_op jit(solution)/shard_map/ppermute | solution.py:59
  12.0 0.7 %collective-permute-start.1 = (bf16[32,2048]{1,0:T(8,128)(2,1)S(1)}, bf16[32,2048]{1,0:T(8,128)(2,1)S(1)}, u32[]{:S(2)}, u32[]{:S(2)}) collective-permute-start(bf16[32,2048]{1,0:T(8,128)(2,1)S(1)} %get-tuple-element.19), channel_id=1, source_target_pairs={{0,32},{16,240},{32,64},{48,16},{64,96},{80,48},{96,128},{112,80},... | collective-permute-start | bytes 393224 | tf_op jit(solution)/shard_map/ppermute | solution.py:59
  12.8 2.2 %collective-permute-done.3.r4_ref = bf16[32,1024]{1,0:T(8,128)(2,1)S(1)} collective-permute-done((bf16[32,1024]{1,0:T(8,128)(2,1)S(1)}, bf16[32,1024]{1,0:T(8,128)(2,1)S(1)}, u32[]{:S(2)}, u32[]{:S(2)}) %collective-permute-start.3) | collective-permute-done | bytes 65568 | tf_op jit(solution)/shard_map/ppermute | solution.py:59
  15.0 3.1 %collective-permute-start.4 = (bf16[32,2048]{1,0:T(8,128)(2,1)S(1)}, bf16[32,2048]{1,0:T(8,128)(2,1)S(1)}, u32[]{:S(2)}, u32[]{:S(2)}) collective-permute-start(bf16[32,2048]{1,0:T(8,128)(2,1)S(1)} %shard_map.105), channel_id=1, source_target_pairs={{0,64},{16,208},{32,96},{48,240},{64,128},{80,16},{96,160},{112,48... | collective-permute-start | bytes 393224 | tf_op jit(solution)/shard_map/ppermute | solution.py:59
  18.2 3.1 %collective-permute-done.4.rm_ref = bf16[32,2048]{1,0:T(8,128)(2,1)S(1)} collective-permute-done((bf16[32,2048]{1,0:T(8,128)(2,1)S(1)}, bf16[32,2048]{1,0:T(8,128)(2,1)S(1)}, u32[]{:S(2)}, u32[]{:S(2)}) %collective-permute-start.4) | collective-permute-done | bytes 131104 | tf_op jit(solution)/shard_map/ppermute | solution.py:59
  21.3 4.4 %collective-permute-start.5 = (bf16[32,2048]{1,0:T(8,128)(2,1)S(1)}, bf16[32,2048]{1,0:T(8,128)(2,1)S(1)}, u32[]{:S(2)}, u32[]{:S(2)}) collective-permute-start(bf16[32,2048]{1,0:T(8,128)(2,1)S(1)} %shard_map.106.t_ref), channel_id=1, source_target_pairs={{0,16},{16,0},{32,48},{48,32},{64,80},{80,64},{96,112},{112,96},{1... | collective-permute-start | bytes 393224 | tf_op jit(solution)/shard_map/ppermute | solution.py:63
  25.8 1.0 %collective-permute-done.5.rt_ref = bf16[32,2048]{1,0:T(8,128)(2,1)S(1)} collective-permute-done((bf16[32,2048]{1,0:T(8,128)(2,1)S(1)}, bf16[32,2048]{1,0:T(8,128)(2,1)S(1)}, u32[]{:S(2)}, u32[]{:S(2)}) %collective-permute-start.5) | collective-permute-done | bytes 131104 | tf_op jit(solution)/shard_map/ppermute | solution.py:63
  26.9 2.0 %collective-permute-start.6 = (bf16[32,2048]{1,0:T(8,128)(2,1)S(1)}, bf16[32,2048]{1,0:T(8,128)(2,1)S(1)}, u32[]{:S(2)}, u32[]{:S(2)}) collective-permute-start(bf16[32,2048]{1,0:T(8,128)(2,1)S(1)} %shard_map.107.n_ref), channel_id=1, source_target_pairs={{0,32},{16,240},{32,64},{48,16},{64,96},{80,48},{96,128},{112,80},... | collective-permute-start | bytes 393224 | tf_op jit(solution)/shard_map/ppermute | solution.py:59
  28.9 3.0 %collective-permute-done.7.g2_ref = bf16[32,2048]{1,0:T(8,128)(2,1)S(1)} collective-permute-done((bf16[32,2048]{1,0:T(8,128)(2,1)S(1)}, bf16[32,2048]{1,0:T(8,128)(2,1)S(1)}, u32[]{:S(2)}, u32[]{:S(2)}) %collective-permute-start.7) | collective-permute-done | bytes 131104 | tf_op jit(solution)/shard_map/ppermute | solution.py:59
  31.9 2.5 %collective-permute-start.9 = (bf16[32,2048]{1,0:T(8,128)(2,1)S(1)}, bf16[32,2048]{1,0:T(8,128)(2,1)S(1)}, u32[]{:S(2)}, u32[]{:S(2)}) collective-permute-start(bf16[32,2048]{1,0:T(8,128)(2,1)S(1)} %collective-permute-done.7.g2_ref), channel_id=1, source_target_pairs={{0,32},{16,240},{32,64},{48,16},{64,96},{80,48},{96,128},{112,80},... | collective-permute-start | bytes 393224 | tf_op jit(solution)/shard_map/ppermute | solution.py:59
  34.4 1.2 %collective-permute-start.10 = (bf16[32,1024]{1,0:T(8,128)(2,1)S(1)}, bf16[32,1024]{1,0:T(8,128)(2,1)S(1)}, u32[]{:S(2)}, u32[]{:S(2)}) collective-permute-start(bf16[32,1024]{1,0:T(8,128)(2,1)S(1)} %get-tuple-element.26), channel_id=1, source_target_pairs={{0,64},{16,208},{32,96},{48,240},{64,128},{80,16},{96,160},{112,48... | collective-permute-start | bytes 196616 | tf_op jit(solution)/shard_map/ppermute | solution.py:59
  35.7 0.7 %collective-permute-start.8 = (bf16[32,4096]{1,0:T(8,128)(2,1)S(1)}, bf16[32,4096]{1,0:T(8,128)(2,1)S(1)}, u32[]{:S(2)}, u32[]{:S(2)}) collective-permute-start(bf16[32,4096]{1,0:T(8,128)(2,1)S(1)} %get-tuple-element.25), channel_id=1, source_target_pairs={{0,16},{16,0},{32,48},{48,32},{64,80},{80,64},{96,112},{112,96},{1... | collective-permute-start | bytes 786440 | tf_op jit(solution)/shard_map/ppermute | solution.py:63
  36.3 3.0 %collective-permute-done.10.g4_ref = bf16[32,1024]{1,0:T(8,128)(2,1)S(1)} collective-permute-done((bf16[32,1024]{1,0:T(8,128)(2,1)S(1)}, bf16[32,1024]{1,0:T(8,128)(2,1)S(1)}, u32[]{:S(2)}, u32[]{:S(2)}) %collective-permute-start.10) | collective-permute-done | bytes 65568 | tf_op jit(solution)/shard_map/ppermute | solution.py:59
  39.3 2.5 %collective-permute-start.11 = (bf16[32,3072]{1,0:T(8,128)(2,1)S(1)}, bf16[32,3072]{1,0:T(8,128)(2,1)S(1)}, u32[]{:S(2)}, u32[]{:S(2)}) collective-permute-start(bf16[32,3072]{1,0:T(8,128)(2,1)S(1)} %pad_maximum_fusion), channel_id=1, source_target_pairs={{0,16},{16,0},{32,48},{48,32},{64,80},{80,64},{96,112},{112,96},{1... | collective-permute-start | bytes 589832 | tf_op jit(solution)/shard_map/ppermute | solution.py:63
  41.9 5.0 %shard_map.109.refs_0_ = bf16[32,1024]{1,0:T(8,128)(2,1)} custom-call(bf16[32,1024]{1,0:T(8,128)(2,1)S(1)} %copy-done.1, bf16[32,512,128]{2,1,0:T(8,128)(2,1)S(1)} %bitcast.5, bf16[32,512,128]{2,1,0:T(8,128)(2,1)} %bitcast.8, s32[32,128]{1,0:T(8,128)S(1)} %broadcast_in_dim.2.len_ref), custom_call_target="tpu_custom_call" | custom-call | flops 200000000 | bytes 4194304 | tf_op jit(solution)/shard_map/pallas_call | solution.py:289
  47.0 4.5 %shard_map.110 = bf16[32,1024]{1,0:T(8,128)(2,1)} custom-call(bf16[32,1024]{1,0:T(8,128)(2,1)S(1)} %copy-done.1, bf16[32,512,128]{2,1,0:T(8,128)(2,1)S(1)} %bitcast.6, bf16[32,512,128]{2,1,0:T(8,128)(2,1)} %bitcast.9, s32[32,128]{1,0:T(8,128)S(1)} %broadcast_in_dim.2.len_ref, bf16[32,1024]{1,0:T(8,128)(2,1)} %shard_map.109.refs_0_), custom_call_target="tpu_custom_call", output_to_operand_aliasing={{}: (4, {})} | custom-call | flops 200000000 | bytes 4194304 | tf_op jit(solution)/shard_map/pallas_call | solution.py:289
  51.4 0.9 %early.1 = (bf16[32,16384]{1,0:T(8,128)(2,1)}, f32[16,32,128]{2,1,0:T(8,128)S(1)}) custom-call(bf16[32,2048]{1,0:T(8,128)(2,1)S(1)} %shard_map.107.n_ref, bf16[32,2048]{1,0:T(8,128)(2,1)S(1)} %collective-permute-done.6.g1_ref, bf16[32,2048]{1,0:T(8,128)(2,1)S(1)} %collective-permute-done.7.g2_ref, bf16[32,4096]{1,0:T(8,128)(2,1)S(1)} %collective-permute-done.8.w12_ref), custom_call_target="tpu_custom_call" | custom-call | flops 1000000 | bytes 1048576 | tf_op jit(solution)/shard_map/early/pallas_call | solution.py:357
  52.3 2.0 %finish.1 = (bf16[32,16384]{1,0:T(8,128)(2,1)}, bf16[32,16384]{1,0:T(8,128)(2,1)}, f32[1,32]{1,0:T(1,128)}) custom-call(bf16[32,2048]{1,0:T(8,128)(2,1)S(1)} %shard_map.107.n_ref, bf16[32,2048]{1,0:T(8,128)(2,1)S(1)} %collective-permute-done.6.g1_ref, bf16[32,2048]{1,0:T(8,128)(2,1)S(1)} %collective-permute-done.7.g2_ref, ...), custom_call_target="tpu_custom_call", output_to_operand_aliasing={{0}: (9, {})} | custom-call | flops 1000000 | bytes 4194304 | tf_op jit(solution)/shard_map/finish/pallas_call | solution.py:367
  (22 shorter events, 0.4 us)
Async XLA Ops:
  0.6 41.2 %copy-start.2 = (bf16[16384]{0:T(1024)(128)(2,1)S(1)}, bf16[16384]{0:T(1024)(128)(2,1)}, u32[]{:S(2)}) copy-start(bf16[16384]{0:T(1024)(128)(2,1)} %param.9) | copy-start | bytes 98308
  0.6 41.2 %copy-start.3 = (s32[32]{0:T(128)S(1)}, s32[32]{0:T(128)}, u32[]{:S(2)}) copy-start(s32[32]{0:T(128)} %param.13) | copy-start | bytes 388
  0.7 41.3 %copy-start = (bf16[1,32,512,128]{3,2,1,0:T(8,128)(2,1)S(1)}, bf16[1,32,512,128]{3,2,1,0:T(8,128)(2,1)}, u32[]{:S(2)}) copy-start(bf16[1,32,512,128]{3,2,1,0:T(8,128)(2,1)} %param.11) | copy-start | bytes 12582916
  0.7 41.3 %copy-start.1 = (bf16[32,1024]{1,0:T(8,128)(2,1)S(1)}, bf16[32,1024]{1,0:T(8,128)(2,1)}, u32[]{:S(2)}) copy-start(bf16[32,1024]{1,0:T(8,128)(2,1)} %q_ref.3) | copy-start | bytes 196612
  2.0 4.8 %collective-permute-start = (bf16[32,8192]{1,0:T(8,128)(2,1)S(1)}, bf16[32,8192]{1,0:T(8,128)(2,1)S(1)}, u32[]{:S(2)}, u32[]{:S(2)}) collective-permute-start(bf16[32,8192]{1,0:T(8,128)(2,1)S(1)} %shard_map.103), channel_id=1, source_target_pairs={{0,16},{16,0},{32,48},{48,32},{64,80},{80,64},{96,112},{112,96},{1... | collective-permute-start | bytes 1572872 | tf_op jit(solution)/shard_map/ppermute | solution.py:63
  6.9 8.1 %collective-permute-start.2 = (bf16[32,2048]{1,0:T(8,128)(2,1)S(1)}, bf16[32,2048]{1,0:T(8,128)(2,1)S(1)}, u32[]{:S(2)}, u32[]{:S(2)}) collective-permute-start(bf16[32,2048]{1,0:T(8,128)(2,1)S(1)} %get-tuple-element.21), channel_id=1, source_target_pairs={{0,32},{16,240},{32,64},{48,16},{64,96},{80,48},{96,128},{112,80},... | collective-permute-start | bytes 393224 | tf_op jit(solution)/shard_map/ppermute | solution.py:59
  10.9 4.1 %collective-permute-start.3 = (bf16[32,1024]{1,0:T(8,128)(2,1)S(1)}, bf16[32,1024]{1,0:T(8,128)(2,1)S(1)}, u32[]{:S(2)}, u32[]{:S(2)}) collective-permute-start(bf16[32,1024]{1,0:T(8,128)(2,1)S(1)} %get-tuple-element.22), channel_id=1, source_target_pairs={{0,64},{16,208},{32,96},{48,240},{64,128},{80,16},{96,160},{112,48... | collective-permute-start | bytes 196616 | tf_op jit(solution)/shard_map/ppermute | solution.py:59
  12.0 6.2 %collective-permute-start.1 = (bf16[32,2048]{1,0:T(8,128)(2,1)S(1)}, bf16[32,2048]{1,0:T(8,128)(2,1)S(1)}, u32[]{:S(2)}, u32[]{:S(2)}) collective-permute-start(bf16[32,2048]{1,0:T(8,128)(2,1)S(1)} %get-tuple-element.19), channel_id=1, source_target_pairs={{0,32},{16,240},{32,64},{48,16},{64,96},{80,48},{96,128},{112,80},... | collective-permute-start | bytes 393224 | tf_op jit(solution)/shard_map/ppermute | solution.py:59
  15.0 6.2 %collective-permute-start.4 = (bf16[32,2048]{1,0:T(8,128)(2,1)S(1)}, bf16[32,2048]{1,0:T(8,128)(2,1)S(1)}, u32[]{:S(2)}, u32[]{:S(2)}) collective-permute-start(bf16[32,2048]{1,0:T(8,128)(2,1)S(1)} %shard_map.105), channel_id=1, source_target_pairs={{0,64},{16,208},{32,96},{48,240},{64,128},{80,16},{96,160},{112,48... | collective-permute-start | bytes 393224 | tf_op jit(solution)/shard_map/ppermute | solution.py:59
  21.3 5.4 %collective-permute-start.5 = (bf16[32,2048]{1,0:T(8,128)(2,1)S(1)}, bf16[32,2048]{1,0:T(8,128)(2,1)S(1)}, u32[]{:S(2)}, u32[]{:S(2)}) collective-permute-start(bf16[32,2048]{1,0:T(8,128)(2,1)S(1)} %shard_map.106.t_ref), channel_id=1, source_target_pairs={{0,16},{16,0},{32,48},{48,32},{64,80},{80,64},{96,112},{112,96},{1... | collective-permute-start | bytes 393224 | tf_op jit(solution)/shard_map/ppermute | solution.py:63
  26.8 5.1 %collective-permute-start.7 = (bf16[32,2048]{1,0:T(8,128)(2,1)S(1)}, bf16[32,2048]{1,0:T(8,128)(2,1)S(1)}, u32[]{:S(2)}, u32[]{:S(2)}) collective-permute-start(bf16[32,2048]{1,0:T(8,128)(2,1)S(1)} %shard_map.107.n_ref), channel_id=1, source_target_pairs={{0,64},{16,208},{32,96},{48,240},{64,128},{80,16},{96,160},{112,48... | collective-permute-start | bytes 393224 | tf_op jit(solution)/shard_map/ppermute | solution.py:59
  26.9 7.5 %collective-permute-start.6 = (bf16[32,2048]{1,0:T(8,128)(2,1)S(1)}, bf16[32,2048]{1,0:T(8,128)(2,1)S(1)}, u32[]{:S(2)}, u32[]{:S(2)}) collective-permute-start(bf16[32,2048]{1,0:T(8,128)(2,1)S(1)} %shard_map.107.n_ref), channel_id=1, source_target_pairs={{0,32},{16,240},{32,64},{48,16},{64,96},{80,48},{96,128},{112,80},... | collective-permute-start | bytes 393224 | tf_op jit(solution)/shard_map/ppermute | solution.py:59
  31.9 7.4 %collective-permute-start.9 = (bf16[32,2048]{1,0:T(8,128)(2,1)S(1)}, bf16[32,2048]{1,0:T(8,128)(2,1)S(1)}, u32[]{:S(2)}, u32[]{:S(2)}) collective-permute-start(bf16[32,2048]{1,0:T(8,128)(2,1)S(1)} %collective-permute-done.7.g2_ref), channel_id=1, source_target_pairs={{0,32},{16,240},{32,64},{48,16},{64,96},{80,48},{96,128},{112,80},... | collective-permute-start | bytes 393224 | tf_op jit(solution)/shard_map/ppermute | solution.py:59
  34.4 4.9 %collective-permute-start.10 = (bf16[32,1024]{1,0:T(8,128)(2,1)S(1)}, bf16[32,1024]{1,0:T(8,128)(2,1)S(1)}, u32[]{:S(2)}, u32[]{:S(2)}) collective-permute-start(bf16[32,1024]{1,0:T(8,128)(2,1)S(1)} %get-tuple-element.26), channel_id=1, source_target_pairs={{0,64},{16,208},{32,96},{48,240},{64,128},{80,16},{96,160},{112,48... | collective-permute-start | bytes 196616 | tf_op jit(solution)/shard_map/ppermute | solution.py:59
  35.7 15.8 %collective-permute-start.8 = (bf16[32,4096]{1,0:T(8,128)(2,1)S(1)}, bf16[32,4096]{1,0:T(8,128)(2,1)S(1)}, u32[]{:S(2)}, u32[]{:S(2)}) collective-permute-start(bf16[32,4096]{1,0:T(8,128)(2,1)S(1)} %get-tuple-element.25), channel_id=1, source_target_pairs={{0,16},{16,0},{32,48},{48,32},{64,80},{80,64},{96,112},{112,96},{1... | collective-permute-start | bytes 786440 | tf_op jit(solution)/shard_map/ppermute | solution.py:63
  39.3 13.0 %collective-permute-start.11 = (bf16[32,3072]{1,0:T(8,128)(2,1)S(1)}, bf16[32,3072]{1,0:T(8,128)(2,1)S(1)}, u32[]{:S(2)}, u32[]{:S(2)}) collective-permute-start(bf16[32,3072]{1,0:T(8,128)(2,1)S(1)} %pad_maximum_fusion), channel_id=1, source_target_pairs={{0,16},{16,0},{32,48},{48,32},{64,80},{80,64},{96,112},{112,96},{1... | collective-permute-start | bytes 589832 | tf_op jit(solution)/shard_map/ppermute | solution.py:63

commit v2 on v1

--- a/solution.py
+++ b/solution.py
@@ -65,10 +65,10 @@
 
 def handled(chip, core, way):
     return [
-        (chunk_at(chip, 4) * CHUNK + core * HALF, HALF),
         (chunk_at(chip, 3 * way) * CHUNK, CHUNK),
         (chunk_at(chip, way) * CHUNK, CHUNK),
         (chunk_at(chip, 2 * way) * CHUNK, CHUNK),
+        (chunk_at(chip, 4) * CHUNK + core * HALF, HALF),
         (chip * CHUNK + core * HALF, HALF),
     ]
 
@@ -106,47 +106,39 @@
         c.wait()
 
 
-def presum_kernel(keep_ref, got_ref, a4_ref, a3_ref, a1_ref, s2_ref, s0_ref):
+def presum_kernel(keep_ref, got_ref, *outs):
     at = 0
-    for out in (a4_ref, a3_ref, a1_ref, s2_ref, s0_ref):
+    for out in outs:
         size = out.shape[1]
         mine = keep_ref[:, at : at + size].astype(f32)
         out[...] = (mine + got_ref[:, at : at + size].astype(f32)).astype(bf16)
         at += size
 
 
-def relay_kernel(s2_ref, r3_ref, r4_ref, m_ref):
+def relay_kernel(s2_ref, r3_ref, m_ref):
+    m_ref[...] = (s2_ref[...].astype(f32) + r3_ref[...].astype(f32)).astype(bf16)
+
+
+def arrive_kernel(r1_ref, rm_ref, r4_ref, own_ref, t_ref):
     _, core, _ = place()
-    for half in range(2):
-        cols = slice(half * HALF, (half + 1) * HALF)
-        both = s2_ref[:, cols].astype(f32) + r3_ref[:, cols].astype(f32)
-        here = jnp.where(core == half, 1.0, 0.0).astype(f32)
-        m_ref[:, cols] = (both + here * r4_ref[...].astype(f32)).astype(bf16)
-
-
-def arrive_kernel(r1_ref, rm_ref, s0_ref, t_ref):
-    _, core, _ = place()
+    extra = r4_ref[...].astype(f32) + own_ref[...].astype(f32)
     for half in range(2):
         cols = slice(half * HALF, (half + 1) * HALF)
         both = r1_ref[:, cols].astype(f32) + rm_ref[:, cols].astype(f32)
-        here = jnp.where(core == half, 1.0, 0.0).astype(f32)
-        t_ref[:, cols] = (both + here * s0_ref[...].astype(f32)).astype(bf16)
-
-
-def hsum_kernel(t_ref, rt_ref, res_ref, n_ref):
+        here = jnp.where(core == half, extra, jnp.zeros_like(extra))
+        t_ref[:, cols] = (both + here).astype(bf16)
+
+
+def hsum_kernel(t_ref, rt_ref, res_ref, n_ref, half_ref):
+    _, core, _ = place()
     total = t_ref[...].astype(f32) + rt_ref[...].astype(f32)
-    n_ref[...] = (res_ref[...].astype(f32) + total).astype(bf16)
-
-
-def fork_kernel(g1_ref, g2_ref, half_ref, both_ref):
-    _, core, _ = place()
-    half_ref[...] = g2_ref[:, columns(core * HALF, HALF)]
-    both_ref[:, :CHUNK] = g1_ref[...]
-    both_ref[:, CHUNK:] = g2_ref[...]
-
-
-def pieces(chip, core, way, n, g1, g2, w12, g3=None, g4=None, w34=None):
-    across_ring = chunk_at(chip, 4) * 2
+    n = (res_ref[...].astype(f32) + total).astype(bf16)
+    n_ref[...] = n
+    half_ref[...] = jnp.where(core == 0, n[:, :HALF], n[:, HALF:])
+
+
+def pieces(chip, core, way, n, g1, g2, w12, last=None, w34=None):
+    opposite = 2 * chunk_at(chip, 4)
     early = [
         (n, 0, 2 * chip, 2),
         (g1, 0, 2 * chunk_at(chip, -way), 2),
@@ -155,10 +147,10 @@
         (w12, CHUNK, 2 * chunk_at(chip, 2 * way), 2),
     ]
     late = [
-        (g3, 0, 2 * chunk_at(chip, -3 * way), 2),
-        (g4, 0, across_ring + core, 1),
+        (last, 0, 2 * chunk_at(chip, -3 * way), 2),
+        (last, CHUNK, opposite + core, 1),
         (w34, 0, 2 * chunk_at(chip, 3 * way), 2),
-        (w34, CHUNK, across_ring + 1 - core, 1),
+        (w34, CHUNK, opposite + 1 - core, 1),
     ]
     return early, late
 
@@ -198,12 +190,10 @@
 
 
 def finish_kernel(
-    n_ref, g1_ref, g2_ref, w12_ref, g3_ref, g4_ref, w34_ref, gain_ref, early_sq, _,
+    n_ref, g1_ref, g2_ref, w12_ref, last_ref, w34_ref, gain_ref, early_sq, _,
     res_out, norm_out, peak_ref, y_ref, sq_ref, res_sems, norm_sems,
 ):
-    early, late = pieces(
-        *place(), n_ref, g1_ref, g2_ref, w12_ref, g3_ref, g4_ref, w34_ref
-    )
+    early, late = pieces(*place(), n_ref, g1_ref, g2_ref, w12_ref, last_ref, w34_ref)
     tokens, features = res_out.shape
     copies = write_out(late, res_out, res_sems)
     sq_ref[...] = early_sq[...]
@@ -235,17 +225,14 @@
 
 
 def attend_kernel(first, q_ref, k_ref, v_ref, len_ref, *refs):
-    o_ref, q_rows, o_rows, stage, values, sem, v_sems = refs[-7:]
+    o_ref, q_rows, o_rows, stage, values, sem, v_sem = refs[-7:]
     seqs, width = stage.shape
     heads = width // HEAD_DIM
     rows = seqs * heads
     context = k_ref.shape[1]
     mine = slice(first, first + seqs)
-    fetched = [
-        pltpu.make_async_copy(v_ref.at[first + i], values.at[i], v_sems.at[i]) for i in range(seqs)
-    ]
-    for copy in fetched:
-        copy.start()
+    fetched = pltpu.make_async_copy(v_ref.at[mine], values, v_sem)
+    fetched.start()
     for h in range(heads):
         cols = slice(h * HEAD_DIM, (h + 1) * HEAD_DIM)
         q_rows[pl.ds(h, seqs, stride=heads), :] = q_ref[mine, cols].astype(f32)
@@ -263,8 +250,8 @@
     scores = jnp.where(live, scores * (1.0 / math.sqrt(HEAD_DIM)), -1e30)
     expo = jnp.exp(scores - jnp.max(scores, axis=0, keepdims=True))
     probs = (expo * (1.0 / jnp.sum(expo, axis=0, keepdims=True))).T
+    fetched.wait()
     for i in range(seqs):
-        fetched[i].wait()
         o_rows[i * heads : (i + 1) * heads, :] = jnp.dot(
             probs[i * heads : (i + 1) * heads, :].astype(bf16),
             values[i],
@@ -297,7 +284,7 @@
                     pltpu.VMEM((seqs // SEQ_GROUPS, width), bf16),
                     pltpu.VMEM((seqs // SEQ_GROUPS, *values.shape[1:]), bf16),
                     pltpu.SemaphoreType.DMA,
-                    pltpu.SemaphoreType.DMA((seqs // SEQ_GROUPS,)),
+                    pltpu.SemaphoreType.DMA,
                 ],
                 input_output_aliases={4: 0} if out else {},
                 cost_estimate=cost(200_000_000, nbytes),
@@ -332,22 +319,22 @@
         keep_kernel, (held(8192), held(CHUNK)), partial, residual,
         in_specs=[ANY, ANY], scratch=[dma((6,))],
     )
-    a4, a3, a1, s2, s0 = call(
-        presum_kernel, (held(HALF), held(CHUNK), held(CHUNK), held(CHUNK), held(HALF)), keep, got
+    a3, a1, s2, a4, own = call(
+        presum_kernel, (held(CHUNK), held(CHUNK), held(CHUNK), held(HALF), held(HALF)), keep, got
     )
-    r4 = along(a4, 2)
     r3 = along(a3, 1)
     r1 = along(a1, 1)
-    m = call(relay_kernel, held(CHUNK), s2, r3, r4)
+    r4 = along(a4, 4)
+    m = call(relay_kernel, held(CHUNK), s2, r3)
     rm = along(m, 2)
-    t = call(arrive_kernel, held(CHUNK), r1, rm, s0)
+    t = call(arrive_kernel, held(CHUNK), r1, rm, r4, own)
     rt = across(t)
-    n = call(hsum_kernel, held(CHUNK), t, rt, res)
+    n, half = call(hsum_kernel, (held(CHUNK), held(HALF)), t, rt, res)
     g2 = along(n, 2)
     g1 = along(n, 1)
-    half, both = call(fork_kernel, (held(HALF), held(2 * CHUNK)), g1, g2)
+    g4 = along(half, 4)
     g3 = along(g2, 1)
-    g4 = along(half, 2)
+    both = jnp.concatenate([g1, g2], axis=1)
     w12 = across(both)
     last = jnp.concatenate([g3, g4], axis=1)
     w34 = across(last)
@@ -367,7 +354,7 @@
     res_out, norm_out, peak = pl.pallas_call(
         finish_kernel,
         out_shape=(whole, whole, jax.ShapeDtypeStruct((1, tokens), f32)),
-        in_specs=[VMEM] * 9 + [ANY],
+        in_specs=[VMEM] * 8 + [ANY],
         out_specs=(ANY, ANY, VMEM),
         scratch_shapes=[
             pltpu.VMEM((tokens, features), bf16),
@@ -375,11 +362,11 @@
             dma((4,)),
             dma((blocks,)),
         ],
-        input_output_aliases={9: 0},
+        input_output_aliases={8: 0},
         cost_estimate=cost(1_000_000, 4 << 20),
         compiler_params=SMALL,
         name="finish",
-    )(*map(near, (n, g1, g2, w12, g3, g4, w34, gains, squares)), begun)
+    )(*map(near, (n, g1, g2, w12, last, w34, gains, squares)), begun)
     return res_out, norm_out, peak.reshape(tokens)
 
 

time: 54.5 us -> 51.7 us (0.949)
  Pallas kernels: 15.2 us -> 12.4 us
  starting transfers between devices: 25.7 us -> 24 us
  waiting for transfers between devices: 12.6 us -> 14.2 us
    pallas_call x2, Pallas kernels: 9.48 us -> 6.71 us  [attend(): pl.pallas_call(functools.partial(attend_kernel, g * (seqs // SEQ_GROUPS))...]
    ppermute x8, waiting for transfers between devices: 11.3 us -> 12.9 us  [along(): return lax.ppermute(x, 'tp', pairs)]
    ppermute x4, starting transfers between devices: 10.9 us -> 9.35 us  [across(): return lax.ppermute(x, 'tp', [(i, i ^ 1) for i in range(2 * CHIPS)])]
    pallas_call x7 -> x6, Pallas kernels: 2.81 us -> 2.77 us  [call(): pl.pallas_call(kernel, out_shape=outs, in_specs=in_specs or [VMEM] * len(...]
  transfers between devices with their start and end apart: 12 -> 12, of which waited for: 6 -> 6; matrix products, arithmetic and copies ran while one was open for 0% -> 0% of each run, Pallas kernels for 21% -> 17%
where the time goes in v2:
time: 51.7 us; the launch traced here: 51.5 us
  starting transfers between devices  24 us (46%)
  waiting for transfers between devices  14.2 us (27%)
  Pallas kernels  12.4 us (24%)
  between operations  0.78 us (2%)
    ppermute x8, starting transfers between devices, along(): return lax.ppermute(x, 'tp', pairs)  14.7 us
    ppermute x8, waiting for transfers between devices, along(): return lax.ppermute(x, 'tp', pairs)  12.9 us
    ppermute x4, starting transfers between devices, across(): return lax.ppermute(x, 'tp', [(i, i ^ 1) for i in range(2 * CHIPS)])  9.35 us
    pallas_call x2, Pallas kernels, attend(): pl.pallas_call(functools.partial(attend_kernel, g * (seqs // SEQ_GROUPS))...  6.71 us
    pallas_call x6, Pallas kernels, call(): pl.pallas_call(kernel, out_shape=outs, in_specs=in_specs or [VMEM] * len(...  2.77 us
    pallas_call x1, Pallas kernels, summed_and_normed(): pl.pallas_call(finish_kernel, out_shape=(whole, whole, jax.ShapeDtypeStru...  2.05 us
    ppermute x4, waiting for transfers between devices, across(): return lax.ppermute(x, 'tp', [(i, i ^ 1) for i in range(2 * CHIPS)])  1.31 us
  transfers between devices with their start and end apart: 12, of which 6 were waited for; matrix products, arithmetic and copies ran while one was open for 0% of the time, Pallas kernels for 17%

profile of v2, /device:TPU:1, one launch (start us, length us, event | category | flops | bytes accessed | tf_op | source)
XLA Modules:
  0.0 51.5 jit_solution(4282600427247689981)
XLA Ops:
  0.7 1.3 %shard_map.103 = bf16[32,8192]{1,0:T(8,128)(2,1)S(1)} custom-call(bf16[32,16384]{1,0:T(8,128)(2,1)} %bitcast.10), custom_call_target="tpu_custom_call" | custom-call | flops 1000 | bytes 1048576 | tf_op jit(solution)/shard_map/pallas_call | solution.py:306
  2.0 3.3 %collective-permute-start = (bf16[32,8192]{1,0:T(8,128)(2,1)S(1)}, bf16[32,8192]{1,0:T(8,128)(2,1)S(1)}, u32[]{:S(2)}, u32[]{:S(2)}) collective-permute-start(bf16[32,8192]{1,0:T(8,128)(2,1)S(1)} %shard_map.103), channel_id=1, source_target_pairs={{0,16},{16,0},{32,48},{48,32},{64,80},{80,64},{96,112},{112,96},{1... | collective-permute-start | bytes 1572872 | tf_op jit(solution)/shard_map/ppermute | solution.py:63
  5.2 1.2 %shard_map.102 = (bf16[32,8192]{1,0:T(8,128)(2,1)S(1)}, bf16[32,2048]{1,0:T(8,128)(2,1)S(1)}) custom-call(bf16[32,16384]{1,0:T(8,128)(2,1)} %bitcast.11, bf16[32,16384]{1,0:T(8,128)(2,1)} %r_ref.1), custom_call_target="tpu_custom_call" | custom-call | flops 1000 | bytes 1048576 | tf_op jit(solution)/shard_map/pallas_call | solution.py:306
  6.5 0.3 collective-permute-done.got_ref
  6.8 0.1 shard_map.104
  6.9 3.9 %collective-permute-start.2 = (bf16[32,2048]{1,0:T(8,128)(2,1)S(1)}, bf16[32,2048]{1,0:T(8,128)(2,1)S(1)}, u32[]{:S(2)}, u32[]{:S(2)}) collective-permute-start(bf16[32,2048]{1,0:T(8,128)(2,1)S(1)} %get-tuple-element.21), channel_id=1, source_target_pairs={{0,32},{16,240},{32,64},{48,16},{64,96},{80,48},{96,128},{112,80},... | collective-permute-start | bytes 393224 | tf_op jit(solution)/shard_map/ppermute | solution.py:59
  10.9 0.7 %collective-permute-start.1 = (bf16[32,2048]{1,0:T(8,128)(2,1)S(1)}, bf16[32,2048]{1,0:T(8,128)(2,1)S(1)}, u32[]{:S(2)}, u32[]{:S(2)}) collective-permute-start(bf16[32,2048]{1,0:T(8,128)(2,1)S(1)} %get-tuple-element.19), channel_id=1, source_target_pairs={{0,32},{16,240},{32,64},{48,16},{64,96},{80,48},{96,128},{112,80},... | collective-permute-start | bytes 393224 | tf_op jit(solution)/shard_map/ppermute | solution.py:59
  11.6 1.2 %collective-permute-done.2.r3_ref = bf16[32,2048]{1,0:T(8,128)(2,1)S(1)} collective-permute-done((bf16[32,2048]{1,0:T(8,128)(2,1)S(1)}, bf16[32,2048]{1,0:T(8,128)(2,1)S(1)}, u32[]{:S(2)}, u32[]{:S(2)}) %collective-permute-start.2) | collective-permute-done | bytes 131104 | tf_op jit(solution)/shard_map/ppermute | solution.py:59
  12.8 2.7 %collective-permute-start.3 = (bf16[32,2048]{1,0:T(8,128)(2,1)S(1)}, bf16[32,2048]{1,0:T(8,128)(2,1)S(1)}, u32[]{:S(2)}, u32[]{:S(2)}) collective-permute-start(bf16[32,2048]{1,0:T(8,128)(2,1)S(1)} %shard_map.105), channel_id=1, source_target_pairs={{0,64},{16,208},{32,96},{48,240},{64,128},{80,16},{96,160},{112,48... | collective-permute-start | bytes 393224 | tf_op jit(solution)/shard_map/ppermute | solution.py:59
  15.5 0.7 %collective-permute-start.4 = (bf16[32,1024]{1,0:T(8,128)(2,1)S(1)}, bf16[32,1024]{1,0:T(8,128)(2,1)S(1)}, u32[]{:S(2)}, u32[]{:S(2)}) collective-permute-start(bf16[32,1024]{1,0:T(8,128)(2,1)S(1)} %get-tuple-element.22), channel_id=1, source_target_pairs={{0,128},{16,144},{32,160},{48,176},{64,192},{80,208},{96,224},{112... | collective-permute-start | bytes 196616 | tf_op jit(solution)/shard_map/ppermute | solution.py:59
  16.2 8.6 %collective-permute-done.4.r4_ref = bf16[32,1024]{1,0:T(8,128)(2,1)S(1)} collective-permute-done((bf16[32,1024]{1,0:T(8,128)(2,1)S(1)}, bf16[32,1024]{1,0:T(8,128)(2,1)S(1)}, u32[]{:S(2)}, u32[]{:S(2)}) %collective-permute-start.4) | collective-permute-done | bytes 65568 | tf_op jit(solution)/shard_map/ppermute | solution.py:59
  24.9 0.5 collective-permute-start.5
  25.3 1.0 %collective-permute-done.5.rt_ref = bf16[32,2048]{1,0:T(8,128)(2,1)S(1)} collective-permute-done((bf16[32,2048]{1,0:T(8,128)(2,1)S(1)}, bf16[32,2048]{1,0:T(8,128)(2,1)S(1)}, u32[]{:S(2)}, u32[]{:S(2)}) %collective-permute-start.5) | collective-permute-done | bytes 131104 | tf_op jit(solution)/shard_map/ppermute | solution.py:63
  26.4 3.7 %collective-permute-start.7 = (bf16[32,2048]{1,0:T(8,128)(2,1)S(1)}, bf16[32,2048]{1,0:T(8,128)(2,1)S(1)}, u32[]{:S(2)}, u32[]{:S(2)}) collective-permute-start(bf16[32,2048]{1,0:T(8,128)(2,1)S(1)} %get-tuple-element.25.n_ref), channel_id=1, source_target_pairs={{0,64},{16,208},{32,96},{48,240},{64,128},{80,16},{96,160},{112,48... | collective-permute-start | bytes 393224 | tf_op jit(solution)/shard_map/ppermute | solution.py:59
  30.1 2.6 %collective-permute-start.10 = (bf16[32,1024]{1,0:T(8,128)(2,1)S(1)}, bf16[32,1024]{1,0:T(8,128)(2,1)S(1)}, u32[]{:S(2)}, u32[]{:S(2)}) collective-permute-start(bf16[32,1024]{1,0:T(8,128)(2,1)S(1)} %get-tuple-element.26), channel_id=1, source_target_pairs={{0,128},{16,144},{32,160},{48,176},{64,192},{80,208},{96,224},{112... | collective-permute-start | bytes 196616 | tf_op jit(solution)/shard_map/ppermute | solution.py:59
  32.7 0.4 collective-permute-start.9
  33.0 0.9 %collective-permute-done.6.g1_ref = bf16[32,2048]{1,0:T(8,128)(2,1)S(1)} collective-permute-done((bf16[32,2048]{1,0:T(8,128)(2,1)S(1)}, bf16[32,2048]{1,0:T(8,128)(2,1)S(1)}, u32[]{:S(2)}, u32[]{:S(2)}) %collective-permute-start.6) | collective-permute-done | bytes 131104 | tf_op jit(solution)/shard_map/ppermute | solution.py:59
  33.9 2.9 %collective-permute-start.8 = (bf16[32,4096]{1,0:T(8,128)(2,1)S(1)}, bf16[32,4096]{1,0:T(8,128)(2,1)S(1)}, u32[]{:S(2)}, u32[]{:S(2)}) collective-permute-start(bf16[32,4096]{1,0:T(8,128)(2,1)S(1)} %pad_maximum_fusion), channel_id=1, source_target_pairs={{0,16},{16,0},{32,48},{48,32},{64,80},{80,64},{96,112},{112,96},{1... | collective-permute-start | bytes 786440 | tf_op jit(solution)/shard_map/ppermute | solution.py:63
  36.8 2.2 %collective-permute-done.9 = bf16[32,2048]{1,0:T(8,128)(2,1)S(1)} collective-permute-done((bf16[32,2048]{1,0:T(8,128)(2,1)S(1)}, bf16[32,2048]{1,0:T(8,128)(2,1)S(1)}, u32[]{:S(2)}, u32[]{:S(2)}) %collective-permute-start.9) | collective-permute-done | bytes 131104 | tf_op jit(solution)/shard_map/ppermute | solution.py:59
  39.1 2.7 %collective-permute-start.11 = (bf16[32,3072]{1,0:T(8,128)(2,1)S(1)}, bf16[32,3072]{1,0:T(8,128)(2,1)S(1)}, u32[]{:S(2)}, u32[]{:S(2)}) collective-permute-start(bf16[32,3072]{1,0:T(8,128)(2,1)S(1)} %constant_dynamic-update-slice_fusion.last_ref), channel_id=1, source_target_pairs={{0,16},{16,0},{32,48},{48,32},{64,80},{80,64},{96,112},{112,96},{1... | collective-permute-start | bytes 589832 | tf_op jit(solution)/shard_map/ppermute | solution.py:63
  41.8 3.8 %shard_map.108.refs_0_ = bf16[32,1024]{1,0:T(8,128)(2,1)} custom-call(bf16[32,1024]{1,0:T(8,128)(2,1)S(1)} %copy-done.1, bf16[32,512,128]{2,1,0:T(8,128)(2,1)S(1)} %bitcast.5, bf16[32,512,128]{2,1,0:T(8,128)(2,1)} %bitcast.8, s32[32,128]{1,0:T(8,128)S(1)} %broadcast_in_dim.2.len_ref), custom_call_target="tpu_custom_call" | custom-call | flops 200000000 | bytes 4194304 | tf_op jit(solution)/shard_map/pallas_call | solution.py:276
  45.7 2.9 %shard_map.109 = bf16[32,1024]{1,0:T(8,128)(2,1)} custom-call(bf16[32,1024]{1,0:T(8,128)(2,1)S(1)} %copy-done.1, bf16[32,512,128]{2,1,0:T(8,128)(2,1)S(1)} %bitcast.6, bf16[32,512,128]{2,1,0:T(8,128)(2,1)} %bitcast.9, s32[32,128]{1,0:T(8,128)S(1)} %broadcast_in_dim.2.len_ref, bf16[32,1024]{1,0:T(8,128)(2,1)} %shard_map.108.refs_0_), custom_call_target="tpu_custom_call", output_to_operand_aliasing={{}: (4, {})} | custom-call | flops 200000000 | bytes 4194304 | tf_op jit(solution)/shard_map/pallas_call | solution.py:276
  48.6 0.9 %early.1 = (bf16[32,16384]{1,0:T(8,128)(2,1)}, f32[16,32,128]{2,1,0:T(8,128)S(1)}) custom-call(bf16[32,2048]{1,0:T(8,128)(2,1)S(1)} %get-tuple-element.25.n_ref, bf16[32,2048]{1,0:T(8,128)(2,1)S(1)} %collective-permute-done.6.g1_ref, bf16[32,2048]{1,0:T(8,128)(2,1)S(1)} %collective-permute-done.7.g2_ref, bf16[32,4096]{1,0:T(8,128)(2,1)S(1)} %collective-permute-done.8.w12_ref), custom_call_target="tpu_custom_call" | custom-call | flops 1000000 | bytes 1048576 | tf_op jit(solution)/shard_map/early/pallas_call | solution.py:344
  49.5 2.0 %finish.1 = (bf16[32,16384]{1,0:T(8,128)(2,1)}, bf16[32,16384]{1,0:T(8,128)(2,1)}, f32[1,32]{1,0:T(1,128)}) custom-call(bf16[32,2048]{1,0:T(8,128)(2,1)S(1)} %get-tuple-element.25.n_ref, bf16[32,2048]{1,0:T(8,128)(2,1)S(1)} %collective-permute-done.6.g1_ref, bf16[32,2048]{1,0:T(8,128)(2,1)S(1)} %collective-permute-done.7.g2_ref, ...), custom_call_target="tpu_custom_call", output_to_operand_aliasing={{0}: (8, {})} | custom-call | flops 1000000 | bytes 4194304 | tf_op jit(solution)/shard_map/finish/pallas_call | solution.py:354
  (23 shorter events, 0.3 us)
Async XLA Ops:
  0.6 41.1 %copy-start.2 = (bf16[16384]{0:T(1024)(128)(2,1)S(1)}, bf16[16384]{0:T(1024)(128)(2,1)}, u32[]{:S(2)}) copy-start(bf16[16384]{0:T(1024)(128)(2,1)} %param.9) | copy-start | bytes 98308
  0.6 41.1 %copy-start.3 = (s32[32]{0:T(128)S(1)}, s32[32]{0:T(128)}, u32[]{:S(2)}) copy-start(s32[32]{0:T(128)} %param.13) | copy-start | bytes 388
  0.7 41.2 %copy-start = (bf16[1,32,512,128]{3,2,1,0:T(8,128)(2,1)S(1)}, bf16[1,32,512,128]{3,2,1,0:T(8,128)(2,1)}, u32[]{:S(2)}) copy-start(bf16[1,32,512,128]{3,2,1,0:T(8,128)(2,1)} %param.11) | copy-start | bytes 12582916
  0.7 41.2 %copy-start.1 = (bf16[32,1024]{1,0:T(8,128)(2,1)S(1)}, bf16[32,1024]{1,0:T(8,128)(2,1)}, u32[]{:S(2)}) copy-start(bf16[32,1024]{1,0:T(8,128)(2,1)} %q_ref.3) | copy-start | bytes 196612
  2.0 4.8 %collective-permute-start = (bf16[32,8192]{1,0:T(8,128)(2,1)S(1)}, bf16[32,8192]{1,0:T(8,128)(2,1)S(1)}, u32[]{:S(2)}, u32[]{:S(2)}) collective-permute-start(bf16[32,8192]{1,0:T(8,128)(2,1)S(1)} %shard_map.103), channel_id=1, source_target_pairs={{0,16},{16,0},{32,48},{48,32},{64,80},{80,64},{96,112},{112,96},{1... | collective-permute-start | bytes 1572872 | tf_op jit(solution)/shard_map/ppermute | solution.py:63
  6.9 5.9 %collective-permute-start.2 = (bf16[32,2048]{1,0:T(8,128)(2,1)S(1)}, bf16[32,2048]{1,0:T(8,128)(2,1)S(1)}, u32[]{:S(2)}, u32[]{:S(2)}) collective-permute-start(bf16[32,2048]{1,0:T(8,128)(2,1)S(1)} %get-tuple-element.21), channel_id=1, source_target_pairs={{0,32},{16,240},{32,64},{48,16},{64,96},{80,48},{96,128},{112,80},... | collective-permute-start | bytes 393224 | tf_op jit(solution)/shard_map/ppermute | solution.py:59
  10.9 13.9 %collective-permute-start.1 = (bf16[32,2048]{1,0:T(8,128)(2,1)S(1)}, bf16[32,2048]{1,0:T(8,128)(2,1)S(1)}, u32[]{:S(2)}, u32[]{:S(2)}) collective-permute-start(bf16[32,2048]{1,0:T(8,128)(2,1)S(1)} %get-tuple-element.19), channel_id=1, source_target_pairs={{0,32},{16,240},{32,64},{48,16},{64,96},{80,48},{96,128},{112,80},... | collective-permute-start | bytes 393224 | tf_op jit(solution)/shard_map/ppermute | solution.py:59
  12.8 12.0 %collective-permute-start.3 = (bf16[32,2048]{1,0:T(8,128)(2,1)S(1)}, bf16[32,2048]{1,0:T(8,128)(2,1)S(1)}, u32[]{:S(2)}, u32[]{:S(2)}) collective-permute-start(bf16[32,2048]{1,0:T(8,128)(2,1)S(1)} %shard_map.105), channel_id=1, source_target_pairs={{0,64},{16,208},{32,96},{48,240},{64,128},{80,16},{96,160},{112,48... | collective-permute-start | bytes 393224 | tf_op jit(solution)/shard_map/ppermute | solution.py:59
  15.5 9.3 %collective-permute-start.4 = (bf16[32,1024]{1,0:T(8,128)(2,1)S(1)}, bf16[32,1024]{1,0:T(8,128)(2,1)S(1)}, u32[]{:S(2)}, u32[]{:S(2)}) collective-permute-start(bf16[32,1024]{1,0:T(8,128)(2,1)S(1)} %get-tuple-element.22), channel_id=1, source_target_pairs={{0,128},{16,144},{32,160},{48,176},{64,192},{80,208},{96,224},{112... | collective-permute-start | bytes 196616 | tf_op jit(solution)/shard_map/ppermute | solution.py:59
  24.9 1.5 %collective-permute-start.5 = (bf16[32,2048]{1,0:T(8,128)(2,1)S(1)}, bf16[32,2048]{1,0:T(8,128)(2,1)S(1)}, u32[]{:S(2)}, u32[]{:S(2)}) collective-permute-start(bf16[32,2048]{1,0:T(8,128)(2,1)S(1)} %shard_map.106.t_ref), channel_id=1, source_target_pairs={{0,16},{16,0},{32,48},{48,32},{64,80},{80,64},{96,112},{112,96},{1... | collective-permute-start | bytes 393224 | tf_op jit(solution)/shard_map/ppermute | solution.py:63
  26.4 6.3 %collective-permute-start.7 = (bf16[32,2048]{1,0:T(8,128)(2,1)S(1)}, bf16[32,2048]{1,0:T(8,128)(2,1)S(1)}, u32[]{:S(2)}, u32[]{:S(2)}) collective-permute-start(bf16[32,2048]{1,0:T(8,128)(2,1)S(1)} %get-tuple-element.25.n_ref), channel_id=1, source_target_pairs={{0,64},{16,208},{32,96},{48,240},{64,128},{80,16},{96,160},{112,48... | collective-permute-start | bytes 393224 | tf_op jit(solution)/shard_map/ppermute | solution.py:59
  30.1 3.8 %collective-permute-start.6 = (bf16[32,2048]{1,0:T(8,128)(2,1)S(1)}, bf16[32,2048]{1,0:T(8,128)(2,1)S(1)}, u32[]{:S(2)}, u32[]{:S(2)}) collective-permute-start(bf16[32,2048]{1,0:T(8,128)(2,1)S(1)} %get-tuple-element.25.n_ref), channel_id=1, source_target_pairs={{0,32},{16,240},{32,64},{48,16},{64,96},{80,48},{96,128},{112,80},... | collective-permute-start | bytes 393224 | tf_op jit(solution)/shard_map/ppermute | solution.py:59
  30.1 9.0 %collective-permute-start.10 = (bf16[32,1024]{1,0:T(8,128)(2,1)S(1)}, bf16[32,1024]{1,0:T(8,128)(2,1)S(1)}, u32[]{:S(2)}, u32[]{:S(2)}) collective-permute-start(bf16[32,1024]{1,0:T(8,128)(2,1)S(1)} %get-tuple-element.26), channel_id=1, source_target_pairs={{0,128},{16,144},{32,160},{48,176},{64,192},{80,208},{96,224},{112... | collective-permute-start | bytes 196616 | tf_op jit(solution)/shard_map/ppermute | solution.py:59
  32.7 6.4 %collective-permute-start.9 = (bf16[32,2048]{1,0:T(8,128)(2,1)S(1)}, bf16[32,2048]{1,0:T(8,128)(2,1)S(1)}, u32[]{:S(2)}, u32[]{:S(2)}) collective-permute-start(bf16[32,2048]{1,0:T(8,128)(2,1)S(1)} %collective-permute-done.7.g2_ref), channel_id=1, source_target_pairs={{0,32},{16,240},{32,64},{48,16},{64,96},{80,48},{96,128},{112,80},... | collective-permute-start | bytes 393224 | tf_op jit(solution)/shard_map/ppermute | solution.py:59
  33.9 14.7 %collective-permute-start.8 = (bf16[32,4096]{1,0:T(8,128)(2,1)S(1)}, bf16[32,4096]{1,0:T(8,128)(2,1)S(1)}, u32[]{:S(2)}, u32[]{:S(2)}) collective-permute-start(bf16[32,4096]{1,0:T(8,128)(2,1)S(1)} %pad_maximum_fusion), channel_id=1, source_target_pairs={{0,16},{16,0},{32,48},{48,32},{64,80},{80,64},{96,112},{112,96},{1... | collective-permute-start | bytes 786440 | tf_op jit(solution)/shard_map/ppermute | solution.py:63
  39.1 10.4 %collective-permute-start.11 = (bf16[32,3072]{1,0:T(8,128)(2,1)S(1)}, bf16[32,3072]{1,0:T(8,128)(2,1)S(1)}, u32[]{:S(2)}, u32[]{:S(2)}) collective-permute-start(bf16[32,3072]{1,0:T(8,128)(2,1)S(1)} %constant_dynamic-update-slice_fusion.last_ref), channel_id=1, source_target_pairs={{0,16},{16,0},{32,48},{48,32},{64,80},{80,64},{96,112},{112,96},{1... | collective-permute-start | bytes 589832 | tf_op jit(solution)/shard_map/ppermute | solution.py:63

commit v3 on v2

--- a/solution.py
+++ b/solution.py
@@ -16,6 +16,7 @@
 SEQ_GROUPS = 2
 
 f32, bf16 = jnp.float32, jnp.bfloat16
+BUSY = 1_000_000_000
 ANY = pl.BlockSpec(memory_space=pl.ANY)
 VMEM = pl.BlockSpec(memory_space=pltpu.VMEM)
 SMALL = pltpu.CompilerParams(vmem_limit_bytes=16 << 20)
@@ -51,11 +52,12 @@
     return pl.CostEstimate(flops=flops, bytes_accessed=nbytes, transcendentals=0)
 
 
-def along(x, hops):
+def along(x, hops, upward=0, cross=False):
     pairs = []
     for chip in range(CHIPS):
-        pairs.append((2 * chip, 2 * ((chip + hops) % CHIPS)))
-        pairs.append((2 * chip + 1, 2 * ((chip - hops) % CHIPS) + 1))
+        for core in range(2):
+            to = (chip + (hops if core == upward else -hops)) % CHIPS
+            pairs.append((2 * chip + core, 2 * to + (1 - core if cross else core)))
     return lax.ppermute(x, "tp", pairs)
 
 
@@ -63,54 +65,54 @@
     return lax.ppermute(x, "tp", [(i, i ^ 1) for i in range(2 * CHIPS)])
 
 
+def first_handled(chip, way):
+    return [(chunk_at(chip, 3 * way) * CHUNK, CHUNK)]
+
+
 def handled(chip, core, way):
     return [
-        (chunk_at(chip, 3 * way) * CHUNK, CHUNK),
         (chunk_at(chip, way) * CHUNK, CHUNK),
-        (chunk_at(chip, 2 * way) * CHUNK, CHUNK),
+        (chunk_at(chip, -2 * way) * CHUNK, CHUNK),
         (chunk_at(chip, 4) * CHUNK + core * HALF, HALF),
         (chip * CHUNK + core * HALF, HALF),
     ]
 
 
-def copy_ranges(src, dst, ranges, sems):
+def fetch(src, dst, ranges, sems):
     copies, at = [], 0
-    for i, (start, size) in enumerate(ranges):
+    for start, size in ranges:
         copies.append(
             pltpu.make_async_copy(
-                src.at[:, columns(start, size)], dst.at[:, pl.ds(at, size)], sems.at[i]
+                src.at[:, columns(start, size)], dst.at[:, pl.ds(at, size)], sems.at[len(copies)]
             )
         )
+        copies[-1].start()
         at += size
     return copies
 
 
+def first_kernel(p_ref, send_ref, keep_ref, send_sems, keep_sems):
+    chip, _, way = place()
+    copies = fetch(p_ref, send_ref, first_handled(chip, -way), send_sems)
+    copies += fetch(p_ref, keep_ref, first_handled(chip, way), keep_sems)
+    for copy in copies:
+        copy.wait()
+
+
 def pack_kernel(p_ref, send_ref, sems):
     chip, core, way = place()
-    copies = copy_ranges(p_ref, send_ref, handled(chip, 1 - core, -way), sems)
-    for c in copies:
-        c.start()
-    for c in copies:
-        c.wait()
-
-
-def keep_kernel(p_ref, r_ref, keep_ref, res_ref, sems):
-    chip, core, way = place()
-    copies = copy_ranges(p_ref, keep_ref, handled(chip, core, way), sems)
-    copies.append(
-        pltpu.make_async_copy(r_ref.at[:, columns(chip * CHUNK, CHUNK)], res_ref, sems.at[5])
-    )
-    for c in copies:
-        c.start()
-    for c in copies:
-        c.wait()
-
-
-def presum_kernel(keep_ref, got_ref, *outs):
+    for copy in fetch(p_ref, send_ref, handled(chip, 1 - core, -way), sems):
+        copy.wait()
+
+
+def first_sum_kernel(keep_ref, got_ref, out_ref):
+    out_ref[...] = (keep_ref[...].astype(f32) + got_ref[...].astype(f32)).astype(bf16)
+
+
+def presum_kernel(p_ref, got_ref, *outs):
     at = 0
-    for out in outs:
-        size = out.shape[1]
-        mine = keep_ref[:, at : at + size].astype(f32)
+    for out, (start, size) in zip(outs, handled(*place())):
+        mine = p_ref[:, columns(start, size)].astype(f32)
         out[...] = (mine + got_ref[:, at : at + size].astype(f32)).astype(bf16)
         at += size
 
@@ -129,10 +131,10 @@
         t_ref[:, cols] = (both + here).astype(bf16)
 
 
-def hsum_kernel(t_ref, rt_ref, res_ref, n_ref, half_ref):
-    _, core, _ = place()
+def hsum_kernel(res_ref, t_ref, rt_ref, n_ref, half_ref):
+    chip, core, _ = place()
     total = t_ref[...].astype(f32) + rt_ref[...].astype(f32)
-    n = (res_ref[...].astype(f32) + total).astype(bf16)
+    n = (res_ref[:, columns(chip * CHUNK, CHUNK)].astype(f32) + total).astype(bf16)
     n_ref[...] = n
     half_ref[...] = jnp.where(core == 0, n[:, :HALF], n[:, HALF:])
 
@@ -147,10 +149,10 @@
         (w12, CHUNK, 2 * chunk_at(chip, 2 * way), 2),
     ]
     late = [
-        (last, 0, 2 * chunk_at(chip, -3 * way), 2),
-        (last, CHUNK, opposite + core, 1),
-        (w34, 0, 2 * chunk_at(chip, 3 * way), 2),
-        (w34, CHUNK, opposite + 1 - core, 1),
+        (last, 0, 2 * chunk_at(chip, 3 * way), 2),
+        (last, CHUNK, opposite + 1 - core, 1),
+        (w34, 0, 2 * chunk_at(chip, -3 * way), 2),
+        (w34, CHUNK, opposite + core, 1),
     ]
     return early, late
 
@@ -191,7 +193,7 @@
 
 def finish_kernel(
     n_ref, g1_ref, g2_ref, w12_ref, last_ref, w34_ref, gain_ref, early_sq, _,
-    res_out, norm_out, peak_ref, y_ref, sq_ref, res_sems, norm_sems,
+    res_out, norm_out, peak_out, peak_ref, y_ref, sq_ref, res_sems, norm_sems, peak_sem,
 ):
     early, late = pieces(*place(), n_ref, g1_ref, g2_ref, w12_ref, last_ref, w34_ref)
     tokens, features = res_out.shape
@@ -220,19 +222,19 @@
         )
         copies[-1].start()
     peak_ref[...] = jnp.max(peak.T, axis=0, keepdims=True)
+    copies.append(pltpu.make_async_copy(peak_ref, peak_out, peak_sem))
+    copies[-1].start()
     for copy in copies:
         copy.wait()
 
 
 def attend_kernel(first, q_ref, k_ref, v_ref, len_ref, *refs):
-    o_ref, q_rows, o_rows, stage, values, sem, v_sem = refs[-7:]
+    o_ref, q_rows, o_rows, stage, sem = refs[-5:]
     seqs, width = stage.shape
     heads = width // HEAD_DIM
     rows = seqs * heads
     context = k_ref.shape[1]
     mine = slice(first, first + seqs)
-    fetched = pltpu.make_async_copy(v_ref.at[mine], values, v_sem)
-    fetched.start()
     for h in range(heads):
         cols = slice(h * HEAD_DIM, (h + 1) * HEAD_DIM)
         q_rows[pl.ds(h, seqs, stride=heads), :] = q_ref[mine, cols].astype(f32)
@@ -250,11 +252,10 @@
     scores = jnp.where(live, scores * (1.0 / math.sqrt(HEAD_DIM)), -1e30)
     expo = jnp.exp(scores - jnp.max(scores, axis=0, keepdims=True))
     probs = (expo * (1.0 / jnp.sum(expo, axis=0, keepdims=True))).T
-    fetched.wait()
     for i in range(seqs):
         o_rows[i * heads : (i + 1) * heads, :] = jnp.dot(
             probs[i * heads : (i + 1) * heads, :].astype(bf16),
-            values[i],
+            v_ref[first + i],
             preferred_element_type=f32,
         )
     for h in range(heads):
@@ -276,20 +277,18 @@
             pl.pallas_call(
                 functools.partial(attend_kernel, g * (seqs // SEQ_GROUPS)),
                 out_shape=jax.ShapeDtypeStruct((seqs, width), bf16),
-                in_specs=[VMEM, VMEM, ANY, VMEM] + [ANY] * len(out),
+                in_specs=[VMEM] * 4 + [ANY] * len(out),
                 out_specs=ANY,
                 scratch_shapes=[
                     pltpu.VMEM((rows, HEAD_DIM), f32),
                     pltpu.VMEM((rows, HEAD_DIM), f32),
                     pltpu.VMEM((seqs // SEQ_GROUPS, width), bf16),
-                    pltpu.VMEM((seqs // SEQ_GROUPS, *values.shape[1:]), bf16),
-                    pltpu.SemaphoreType.DMA,
                     pltpu.SemaphoreType.DMA,
                 ],
                 input_output_aliases={4: 0} if out else {},
                 cost_estimate=cost(200_000_000, nbytes),
                 compiler_params=SMALL,
-            )(queries, keys, far(values), near(lens), *out)
+            )(queries, keys, values, near(lens), *out)
         ]
     return out[0]
 
@@ -301,8 +300,8 @@
     def held(width):
         return onchip((tokens, width), bf16)
 
-    def call(kernel, outs, *args, in_specs=None, scratch=(), flops=1000):
-        args = [far(a) if in_specs else near(a) for a in args]
+    def call(kernel, outs, *args, in_specs=None, loose=0, scratch=(), flops=BUSY):
+        args = [far(a) if in_specs else near(a) if i >= loose else a for i, a in enumerate(args)]
         return pl.pallas_call(
             kernel,
             out_shape=outs,
@@ -313,27 +312,29 @@
             compiler_params=SMALL,
         )(*args)
 
-    send = call(pack_kernel, held(8192), partial, in_specs=[ANY], scratch=[dma((5,))])
+    send, keep = call(
+        first_kernel, (held(CHUNK), held(CHUNK)), partial,
+        in_specs=[ANY], scratch=[dma((1,)), dma((1,))], flops=4 * BUSY,
+    )
     got = across(send)
-    keep, res = call(
-        keep_kernel, (held(8192), held(CHUNK)), partial, residual,
-        in_specs=[ANY, ANY], scratch=[dma((6,))],
+    send = call(pack_kernel, held(3 * CHUNK), partial, loose=1, scratch=[dma((4,))], flops=4 * BUSY)
+    got_rest = across(send)
+    a3 = call(first_sum_kernel, held(CHUNK), keep, got)
+    r3 = along(a3, 1, cross=True)
+    a1, s2, a4, own = call(
+        presum_kernel, (held(CHUNK), held(CHUNK), held(HALF), held(HALF)), partial, got_rest, loose=1
     )
-    a3, a1, s2, a4, own = call(
-        presum_kernel, (held(CHUNK), held(CHUNK), held(CHUNK), held(HALF), held(HALF)), keep, got
-    )
-    r3 = along(a3, 1)
     r1 = along(a1, 1)
     r4 = along(a4, 4)
     m = call(relay_kernel, held(CHUNK), s2, r3)
-    rm = along(m, 2)
+    rm = along(m, 2, upward=1, cross=True)
     t = call(arrive_kernel, held(CHUNK), r1, rm, r4, own)
     rt = across(t)
-    n, half = call(hsum_kernel, (held(CHUNK), held(HALF)), t, rt, res)
-    g2 = along(n, 2)
+    n, half = call(hsum_kernel, (held(CHUNK), held(HALF)), residual, t, rt, loose=1)
+    g2 = along(n, 2, upward=1, cross=True)
     g1 = along(n, 1)
-    g4 = along(half, 4)
-    g3 = along(g2, 1)
+    g4 = along(half, 4, cross=True)
+    g3 = along(g2, 1, cross=True)
     both = jnp.concatenate([g1, g2], axis=1)
     w12 = across(both)
     last = jnp.concatenate([g3, g4], axis=1)
@@ -355,12 +356,14 @@
         finish_kernel,
         out_shape=(whole, whole, jax.ShapeDtypeStruct((1, tokens), f32)),
         in_specs=[VMEM] * 8 + [ANY],
-        out_specs=(ANY, ANY, VMEM),
+        out_specs=(ANY, ANY, ANY),
         scratch_shapes=[
+            pltpu.VMEM((1, tokens), f32),
             pltpu.VMEM((tokens, features), bf16),
             pltpu.VMEM((blocks, tokens, 128), f32),
             dma((4,)),
             dma((blocks,)),
+            dma,
         ],
         input_output_aliases={8: 0},
         cost_estimate=cost(1_000_000, 4 << 20),

time: 51.7 us -> 50.6 us (0.979)
  Pallas kernels: 12.4 us -> 8.9 us
  waiting for transfers between devices: 14.2 us -> 16 us
  local copies, waits for them, and re-layouts: 0.1 us -> 1.35 us
  starting transfers between devices: 24 us -> 23.4 us
    ppermute x4 -> x5, starting transfers between devices: 9.35 us -> 6.93 us  [across(): return lax.ppermute(x, 'tp', [(i, i ^ 1) for i in range(2 * CHIPS)])]
    ppermute x8, starting transfers between devices: 14.7 us -> 16.4 us  [along(): return lax.ppermute(x, 'tp', pairs)]
    pallas_call x2, Pallas kernels: 6.71 us -> 5.01 us  [attend(): pl.pallas_call(functools.partial(attend_kernel, g * (seqs // SEQ_GROUPS))...]
    pallas_call x6 -> x7, Pallas kernels: 2.77 us -> 1.45 us  [call(): pl.pallas_call(kernel, out_shape=outs, in_specs=in_specs or [VMEM] * len(...]
    unnamed x9 -> x17, local copies, waits for them, and re-layouts: 0.03 us -> 1.27 us
    ppermute x4 -> x5, waiting for transfers between devices: 1.31 us -> 2.24 us  [across(): return lax.ppermute(x, 'tp', [(i, i ^ 1) for i in range(2 * CHIPS)])]
    ppermute x8, waiting for transfers between devices: 12.9 us -> 13.8 us  [along(): return lax.ppermute(x, 'tp', pairs)]
  transfers between devices with their start and end apart: 12 -> 13, of which waited for: 6 -> 7; matrix products, arithmetic and copies ran while one was open for 0% -> 0% of each run, Pallas kernels for 17% -> 14%
where the time goes in v3:
time: 50.6 us; the launch traced here: 50.5 us
  starting transfers between devices  23.4 us (46%)
  waiting for transfers between devices  16 us (32%)
  Pallas kernels  8.9 us (18%)
  local copies, waits for them, and re-layouts  1.35 us (3%)
  between operations  0.84 us (2%)
    ppermute x8, starting transfers between devices, along(): return lax.ppermute(x, 'tp', pairs)  16.4 us
    ppermute x8, waiting for transfers between devices, along(): return lax.ppermute(x, 'tp', pairs)  13.8 us
    ppermute x5, starting transfers between devices, across(): return lax.ppermute(x, 'tp', [(i, i ^ 1) for i in range(2 * CHIPS)])  6.93 us
    pallas_call x2, Pallas kernels, attend(): pl.pallas_call(functools.partial(attend_kernel, g * (seqs // SEQ_GROUPS))...  5.01 us
    ppermute x5, waiting for transfers between devices, across(): return lax.ppermute(x, 'tp', [(i, i ^ 1) for i in range(2 * CHIPS)])  2.24 us
    pallas_call x1, Pallas kernels, summed_and_normed(): pl.pallas_call(finish_kernel, out_shape=(whole, whole, jax.ShapeDtypeStru...  1.55 us
    pallas_call x7, Pallas kernels, call(): pl.pallas_call(kernel, out_shape=outs, in_specs=in_specs or [VMEM] * len(...  1.45 us
    unnamed x17, local copies, waits for them, and re-layouts  1.27 us
  transfers between devices with their start and end apart: 13, of which 7 were waited for; matrix products, arithmetic and copies ran while one was open for 0% of the time, Pallas kernels for 14%

profile of v3, /device:TPU:1, one launch (start us, length us, event | category | flops | bytes accessed | tf_op | source)
XLA Modules:
  0.0 50.5 jit_solution(13120901141557926926)
XLA Ops:
  0.6 1.2 %copy-done.3 = bf16[1,32,16384]{2,1,0:T(8,128)(2,1)S(1)} copy-done((bf16[1,32,16384]{2,1,0:T(8,128)(2,1)S(1)}, bf16[1,32,16384]{2,1,0:T(8,128)(2,1)}, u32[]{:S(2)}) %copy-start.3) | copy-done | bytes 1048600
  2.0 3.3 %collective-permute-start = (bf16[32,6144]{1,0:T(8,128)(2,1)S(1)}, bf16[32,6144]{1,0:T(8,128)(2,1)S(1)}, u32[]{:S(2)}, u32[]{:S(2)}) collective-permute-start(bf16[32,6144]{1,0:T(8,128)(2,1)S(1)} %shard_map.102), channel_id=1, source_target_pairs={{0,16},{16,0},{32,48},{48,32},{64,80},{80,64},{96,112},{112,96},{1... | collective-permute-start | bytes 1179656 | tf_op jit(solution)/shard_map/ppermute | solution.py:65
  5.3 1.0 %shard_map.104 = (bf16[32,2048]{1,0:T(8,128)(2,1)S(1)}, bf16[32,2048]{1,0:T(8,128)(2,1)S(1)}) custom-call(bf16[32,16384]{1,0:T(8,128)(2,1)} %bitcast.10), custom_call_target="tpu_custom_call" | custom-call | flops 4000000000 | bytes 1048576 | tf_op jit(solution)/shard_map/pallas_call | solution.py:305
  6.3 0.2 collective-permute-start.2
  6.5 1.2 %collective-permute-done.2.got_ref = bf16[32,2048]{1,0:T(8,128)(2,1)S(1)} collective-permute-done((bf16[32,2048]{1,0:T(8,128)(2,1)S(1)}, bf16[32,2048]{1,0:T(8,128)(2,1)S(1)}, u32[]{:S(2)}, u32[]{:S(2)}) %collective-permute-start.2) | collective-permute-done | bytes 131104 | tf_op jit(solution)/shard_map/ppermute | solution.py:65
  7.8 4.0 %collective-permute-start.3 = (bf16[32,2048]{1,0:T(8,128)(2,1)S(1)}, bf16[32,2048]{1,0:T(8,128)(2,1)S(1)}, u32[]{:S(2)}, u32[]{:S(2)}) collective-permute-start(bf16[32,2048]{1,0:T(8,128)(2,1)S(1)} %shard_map.105), channel_id=1, source_target_pairs={{0,48},{16,224},{32,80},{48,0},{64,112},{80,32},{96,144},{112,64},... | collective-permute-start | bytes 393224 | tf_op jit(solution)/shard_map/ppermute | solution.py:61
  11.9 2.5 %collective-permute-done.3.r3_ref = bf16[32,2048]{1,0:T(8,128)(2,1)S(1)} collective-permute-done((bf16[32,2048]{1,0:T(8,128)(2,1)S(1)}, bf16[32,2048]{1,0:T(8,128)(2,1)S(1)}, u32[]{:S(2)}, u32[]{:S(2)}) %collective-permute-start.3) | collective-permute-done | bytes 131104 | tf_op jit(solution)/shard_map/ppermute | solution.py:61
  14.6 2.1 %collective-permute-start.1 = (bf16[32,2048]{1,0:T(8,128)(2,1)S(1)}, bf16[32,2048]{1,0:T(8,128)(2,1)S(1)}, u32[]{:S(2)}, u32[]{:S(2)}) collective-permute-start(bf16[32,2048]{1,0:T(8,128)(2,1)S(1)} %get-tuple-element.17), channel_id=1, source_target_pairs={{0,32},{16,240},{32,64},{48,16},{64,96},{80,48},{96,128},{112,80},... | collective-permute-start | bytes 393224 | tf_op jit(solution)/shard_map/ppermute | solution.py:61
  16.7 4.1 %collective-permute-start.5 = (bf16[32,1024]{1,0:T(8,128)(2,1)S(1)}, bf16[32,1024]{1,0:T(8,128)(2,1)S(1)}, u32[]{:S(2)}, u32[]{:S(2)}) collective-permute-start(bf16[32,1024]{1,0:T(8,128)(2,1)S(1)} %get-tuple-element.21), channel_id=1, source_target_pairs={{0,128},{16,144},{32,160},{48,176},{64,192},{80,208},{96,224},{112... | collective-permute-start | bytes 196616 | tf_op jit(solution)/shard_map/ppermute | solution.py:61
  20.8 3.9 %collective-permute-done.5.r4_ref = bf16[32,1024]{1,0:T(8,128)(2,1)S(1)} collective-permute-done((bf16[32,1024]{1,0:T(8,128)(2,1)S(1)}, bf16[32,1024]{1,0:T(8,128)(2,1)S(1)}, u32[]{:S(2)}, u32[]{:S(2)}) %collective-permute-start.5) | collective-permute-done | bytes 65568 | tf_op jit(solution)/shard_map/ppermute | solution.py:61
  24.8 2.1 %collective-permute-start.6 = (bf16[32,2048]{1,0:T(8,128)(2,1)S(1)}, bf16[32,2048]{1,0:T(8,128)(2,1)S(1)}, u32[]{:S(2)}, u32[]{:S(2)}) collective-permute-start(bf16[32,2048]{1,0:T(8,128)(2,1)S(1)} %shard_map.107.t_ref), channel_id=1, source_target_pairs={{0,16},{16,0},{32,48},{48,32},{64,80},{80,64},{96,112},{112,96},{1... | collective-permute-start | bytes 393224 | tf_op jit(solution)/shard_map/ppermute | solution.py:65
  26.9 1.0 %collective-permute-done.6.rt_ref = bf16[32,2048]{1,0:T(8,128)(2,1)S(1)} collective-permute-done((bf16[32,2048]{1,0:T(8,128)(2,1)S(1)}, bf16[32,2048]{1,0:T(8,128)(2,1)S(1)}, u32[]{:S(2)}, u32[]{:S(2)}) %collective-permute-start.6) | collective-permute-done | bytes 131104 | tf_op jit(solution)/shard_map/ppermute | solution.py:65
  28.0 2.6 %collective-permute-start.8 = (bf16[32,2048]{1,0:T(8,128)(2,1)S(1)}, bf16[32,2048]{1,0:T(8,128)(2,1)S(1)}, u32[]{:S(2)}, u32[]{:S(2)}) collective-permute-start(bf16[32,2048]{1,0:T(8,128)(2,1)S(1)} %get-tuple-element.23.n_ref), channel_id=1, source_target_pairs={{0,208},{16,64},{32,240},{48,96},{64,16},{80,128},{96,48},{112,160... | collective-permute-start | bytes 393224 | tf_op jit(solution)/shard_map/ppermute | solution.py:61
  30.6 1.7 %collective-permute-start.7 = (bf16[32,2048]{1,0:T(8,128)(2,1)S(1)}, bf16[32,2048]{1,0:T(8,128)(2,1)S(1)}, u32[]{:S(2)}, u32[]{:S(2)}) collective-permute-start(bf16[32,2048]{1,0:T(8,128)(2,1)S(1)} %get-tuple-element.23.n_ref), channel_id=1, source_target_pairs={{0,32},{16,240},{32,64},{48,16},{64,96},{80,48},{96,128},{112,80},... | collective-permute-start | bytes 393224 | tf_op jit(solution)/shard_map/ppermute | solution.py:61
  32.3 1.6 %collective-permute-start.11 = (bf16[32,1024]{1,0:T(8,128)(2,1)S(1)}, bf16[32,1024]{1,0:T(8,128)(2,1)S(1)}, u32[]{:S(2)}, u32[]{:S(2)}) collective-permute-start(bf16[32,1024]{1,0:T(8,128)(2,1)S(1)} %get-tuple-element.24), channel_id=1, source_target_pairs={{0,144},{16,128},{32,176},{48,160},{64,208},{80,192},{96,240},{112... | collective-permute-start | bytes 196616 | tf_op jit(solution)/shard_map/ppermute | solution.py:61
  33.9 2.5 %collective-permute-done.8.g2_ref = bf16[32,2048]{1,0:T(8,128)(2,1)S(1)} collective-permute-done((bf16[32,2048]{1,0:T(8,128)(2,1)S(1)}, bf16[32,2048]{1,0:T(8,128)(2,1)S(1)}, u32[]{:S(2)}, u32[]{:S(2)}) %collective-permute-start.8) | collective-permute-done | bytes 131104 | tf_op jit(solution)/shard_map/ppermute | solution.py:61
  36.4 0.2 collective-permute-start.10
  36.6 2.3 %collective-permute-done.7.g1_ref = bf16[32,2048]{1,0:T(8,128)(2,1)S(1)} collective-permute-done((bf16[32,2048]{1,0:T(8,128)(2,1)S(1)}, bf16[32,2048]{1,0:T(8,128)(2,1)S(1)}, u32[]{:S(2)}, u32[]{:S(2)}) %collective-permute-start.7) | collective-permute-done | bytes 131104 | tf_op jit(solution)/shard_map/ppermute | solution.py:61
  38.9 1.2 %collective-permute-start.9 = (bf16[32,4096]{1,0:T(8,128)(2,1)S(1)}, bf16[32,4096]{1,0:T(8,128)(2,1)S(1)}, u32[]{:S(2)}, u32[]{:S(2)}) collective-permute-start(bf16[32,4096]{1,0:T(8,128)(2,1)S(1)} %pad_maximum_fusion), channel_id=1, source_target_pairs={{0,16},{16,0},{32,48},{48,32},{64,80},{80,64},{96,112},{112,96},{1... | collective-permute-start | bytes 786440 | tf_op jit(solution)/shard_map/ppermute | solution.py:65
  40.2 2.6 %collective-permute-done.10 = bf16[32,2048]{1,0:T(8,128)(2,1)S(1)} collective-permute-done((bf16[32,2048]{1,0:T(8,128)(2,1)S(1)}, bf16[32,2048]{1,0:T(8,128)(2,1)S(1)}, u32[]{:S(2)}, u32[]{:S(2)}) %collective-permute-start.10) | collective-permute-done | bytes 131104 | tf_op jit(solution)/shard_map/ppermute | solution.py:61
  43.0 2.5 %shard_map.109.refs_0_ = bf16[32,1024]{1,0:T(8,128)(2,1)} custom-call(bf16[32,1024]{1,0:T(8,128)(2,1)S(1)} %copy-done.2, bf16[32,512,128]{2,1,0:T(8,128)(2,1)S(1)} %bitcast.5, bf16[32,512,128]{2,1,0:T(8,128)(2,1)S(1)} %bitcast.7, s32[32,128]{1,0:T(8,128)S(1)} %broadcast_in_dim.2.len_ref), custom_call_target="tpu_custom_call" | custom-call | flops 200000000 | bytes 4194304 | tf_op jit(solution)/shard_map/pallas_call | solution.py:277
  45.5 2.5 %shard_map.110 = bf16[32,1024]{1,0:T(8,128)(2,1)} custom-call(bf16[32,1024]{1,0:T(8,128)(2,1)S(1)} %copy-done.2, bf16[32,512,128]{2,1,0:T(8,128)(2,1)S(1)} %bitcast.6, bf16[32,512,128]{2,1,0:T(8,128)(2,1)S(1)} %bitcast.8, s32[32,128]{1,0:T(8,128)S(1)} %broadcast_in_dim.2.len_ref, bf16[32,1024]{1,0:T(8,128)(2,1)} %shard_map.109.refs_0_), custom_call_target="tpu_custom_call", output_to_operand_aliasing={{}: (4, {})} | custom-call | flops 200000000 | bytes 4194304 | tf_op jit(solution)/shard_map/pallas_call | solution.py:277
  48.0 0.9 %early.1 = (bf16[32,16384]{1,0:T(8,128)(2,1)}, f32[16,32,128]{2,1,0:T(8,128)S(1)}) custom-call(bf16[32,2048]{1,0:T(8,128)(2,1)S(1)} %get-tuple-element.23.n_ref, bf16[32,2048]{1,0:T(8,128)(2,1)S(1)} %collective-permute-done.7.g1_ref, bf16[32,2048]{1,0:T(8,128)(2,1)S(1)} %collective-permute-done.8.g2_ref, bf16[32,4096]{1,0:T(8,128)(2,1)S(1)} %collective-permute-done.9.w12_ref), custom_call_target="tpu_custom_call" | custom-call | flops 1000000 | bytes 1048576 | tf_op jit(solution)/shard_map/early/pallas_call | solution.py:345
  48.9 1.5 %finish.1 = (bf16[32,16384]{1,0:T(8,128)(2,1)}, bf16[32,16384]{1,0:T(8,128)(2,1)}, f32[1,32]{1,0:T(1,128)}) custom-call(bf16[32,2048]{1,0:T(8,128)(2,1)S(1)} %get-tuple-element.23.n_ref, bf16[32,2048]{1,0:T(8,128)(2,1)S(1)} %collective-permute-done.7.g1_ref, bf16[32,2048]{1,0:T(8,128)(2,1)S(1)} %collective-permute-done.8.g2_ref, ...), custom_call_target="tpu_custom_call", output_to_operand_aliasing={{0}: (8, {})} | custom-call | flops 1000000 | bytes 4194304 | tf_op jit(solution)/shard_map/finish/pallas_call | solution.py:355
  (34 shorter events, 0.8 us)
Async XLA Ops:
  0.6 1.2 %copy-start.3 = (bf16[1,32,16384]{2,1,0:T(8,128)(2,1)S(1)}, bf16[1,32,16384]{2,1,0:T(8,128)(2,1)}, u32[]{:S(2)}) copy-start(bf16[1,32,16384]{2,1,0:T(8,128)(2,1)} %param.7) | copy-start | bytes 3145732
  2.0 9.8 %copy-start.4 = (bf16[1,32,16384]{2,1,0:T(8,128)(2,1)S(1)}, bf16[1,32,16384]{2,1,0:T(8,128)(2,1)}, u32[]{:S(2)}) copy-start(bf16[1,32,16384]{2,1,0:T(8,128)(2,1)} %param.7) | copy-start | bytes 3145732
  2.0 9.7 %collective-permute-start = (bf16[32,6144]{1,0:T(8,128)(2,1)S(1)}, bf16[32,6144]{1,0:T(8,128)(2,1)S(1)}, u32[]{:S(2)}, u32[]{:S(2)}) collective-permute-start(bf16[32,6144]{1,0:T(8,128)(2,1)S(1)} %shard_map.102), channel_id=1, source_target_pairs={{0,16},{16,0},{32,48},{48,32},{64,80},{80,64},{96,112},{112,96},{1... | collective-permute-start | bytes 1179656 | tf_op jit(solution)/shard_map/ppermute | solution.py:65
  6.3 1.4 %collective-permute-start.2 = (bf16[32,2048]{1,0:T(8,128)(2,1)S(1)}, bf16[32,2048]{1,0:T(8,128)(2,1)S(1)}, u32[]{:S(2)}, u32[]{:S(2)}) collective-permute-start(bf16[32,2048]{1,0:T(8,128)(2,1)S(1)} %get-tuple-element.20), channel_id=1, source_target_pairs={{0,16},{16,0},{32,48},{48,32},{64,80},{80,64},{96,112},{112,96},{1... | collective-permute-start | bytes 393224 | tf_op jit(solution)/shard_map/ppermute | solution.py:65
  7.8 6.6 %collective-permute-start.3 = (bf16[32,2048]{1,0:T(8,128)(2,1)S(1)}, bf16[32,2048]{1,0:T(8,128)(2,1)S(1)}, u32[]{:S(2)}, u32[]{:S(2)}) collective-permute-start(bf16[32,2048]{1,0:T(8,128)(2,1)S(1)} %shard_map.105), channel_id=1, source_target_pairs={{0,48},{16,224},{32,80},{48,0},{64,112},{80,32},{96,144},{112,64},... | collective-permute-start | bytes 393224 | tf_op jit(solution)/shard_map/ppermute | solution.py:61
  11.9 16.0 %copy-start.5 = (bf16[32,16384]{1,0:T(8,128)(2,1)S(1)}, bf16[32,16384]{1,0:T(8,128)(2,1)}, u32[]{:S(2)}) copy-start(bf16[32,16384]{1,0:T(8,128)(2,1)} %res_ref.1) | copy-start | bytes 3145732
  14.4 28.6 %copy-start.2 = (bf16[32,1024]{1,0:T(8,128)(2,1)S(1)}, bf16[32,1024]{1,0:T(8,128)(2,1)}, u32[]{:S(2)}) copy-start(bf16[32,1024]{1,0:T(8,128)(2,1)} %q_ref.3) | copy-start | bytes 196612
  14.5 28.4 %copy-start.6 = (bf16[16384]{0:T(1024)(128)(2,1)S(1)}, bf16[16384]{0:T(1024)(128)(2,1)}, u32[]{:S(2)}) copy-start(bf16[16384]{0:T(1024)(128)(2,1)} %param.9) | copy-start | bytes 98308
  14.5 10.2 %collective-permute-start.4 = (bf16[32,2048]{1,0:T(8,128)(2,1)S(1)}, bf16[32,2048]{1,0:T(8,128)(2,1)S(1)}, u32[]{:S(2)}, u32[]{:S(2)}) collective-permute-start(bf16[32,2048]{1,0:T(8,128)(2,1)S(1)} %shard_map.106), channel_id=1, source_target_pairs={{0,208},{16,64},{32,240},{48,96},{64,16},{80,128},{96,48},{112,160... | collective-permute-start | bytes 393224 | tf_op jit(solution)/shard_map/ppermute | solution.py:61
  14.6 10.1 %collective-permute-start.1 = (bf16[32,2048]{1,0:T(8,128)(2,1)S(1)}, bf16[32,2048]{1,0:T(8,128)(2,1)S(1)}, u32[]{:S(2)}, u32[]{:S(2)}) collective-permute-start(bf16[32,2048]{1,0:T(8,128)(2,1)S(1)} %get-tuple-element.17), channel_id=1, source_target_pairs={{0,32},{16,240},{32,64},{48,16},{64,96},{80,48},{96,128},{112,80},... | collective-permute-start | bytes 393224 | tf_op jit(solution)/shard_map/ppermute | solution.py:61
  16.7 8.0 %collective-permute-start.5 = (bf16[32,1024]{1,0:T(8,128)(2,1)S(1)}, bf16[32,1024]{1,0:T(8,128)(2,1)S(1)}, u32[]{:S(2)}, u32[]{:S(2)}) collective-permute-start(bf16[32,1024]{1,0:T(8,128)(2,1)S(1)} %get-tuple-element.21), channel_id=1, source_target_pairs={{0,128},{16,144},{32,160},{48,176},{64,192},{80,208},{96,224},{112... | collective-permute-start | bytes 196616 | tf_op jit(solution)/shard_map/ppermute | solution.py:61
  24.7 18.2 %copy-start.7 = (s32[32]{0:T(128)S(1)}, s32[32]{0:T(128)}, u32[]{:S(2)}) copy-start(s32[32]{0:T(128)} %param.13) | copy-start | bytes 388
  24.7 18.3 %copy-start = (bf16[1,32,512,128]{3,2,1,0:T(8,128)(2,1)S(1)}, bf16[1,32,512,128]{3,2,1,0:T(8,128)(2,1)}, u32[]{:S(2)}) copy-start(bf16[1,32,512,128]{3,2,1,0:T(8,128)(2,1)} %param.11) | copy-start | bytes 12582916
  24.7 18.3 %copy-start.1 = (bf16[1,32,512,128]{3,2,1,0:T(8,128)(2,1)S(1)}, bf16[1,32,512,128]{3,2,1,0:T(8,128)(2,1)}, u32[]{:S(2)}) copy-start(bf16[1,32,512,128]{3,2,1,0:T(8,128)(2,1)} %param.12) | copy-start | bytes 12582916
  24.8 3.1 %collective-permute-start.6 = (bf16[32,2048]{1,0:T(8,128)(2,1)S(1)}, bf16[32,2048]{1,0:T(8,128)(2,1)S(1)}, u32[]{:S(2)}, u32[]{:S(2)}) collective-permute-start(bf16[32,2048]{1,0:T(8,128)(2,1)S(1)} %shard_map.107.t_ref), channel_id=1, source_target_pairs={{0,16},{16,0},{32,48},{48,32},{64,80},{80,64},{96,112},{112,96},{1... | collective-permute-start | bytes 393224 | tf_op jit(solution)/shard_map/ppermute | solution.py:65
  28.0 8.4 %collective-permute-start.8 = (bf16[32,2048]{1,0:T(8,128)(2,1)S(1)}, bf16[32,2048]{1,0:T(8,128)(2,1)S(1)}, u32[]{:S(2)}, u32[]{:S(2)}) collective-permute-start(bf16[32,2048]{1,0:T(8,128)(2,1)S(1)} %get-tuple-element.23.n_ref), channel_id=1, source_target_pairs={{0,208},{16,64},{32,240},{48,96},{64,16},{80,128},{96,48},{112,160... | collective-permute-start | bytes 393224 | tf_op jit(solution)/shard_map/ppermute | solution.py:61
  30.6 8.3 %collective-permute-start.7 = (bf16[32,2048]{1,0:T(8,128)(2,1)S(1)}, bf16[32,2048]{1,0:T(8,128)(2,1)S(1)}, u32[]{:S(2)}, u32[]{:S(2)}) collective-permute-start(bf16[32,2048]{1,0:T(8,128)(2,1)S(1)} %get-tuple-element.23.n_ref), channel_id=1, source_target_pairs={{0,32},{16,240},{32,64},{48,16},{64,96},{80,48},{96,128},{112,80},... | collective-permute-start | bytes 393224 | tf_op jit(solution)/shard_map/ppermute | solution.py:61
  32.3 10.5 %collective-permute-start.11 = (bf16[32,1024]{1,0:T(8,128)(2,1)S(1)}, bf16[32,1024]{1,0:T(8,128)(2,1)S(1)}, u32[]{:S(2)}, u32[]{:S(2)}) collective-permute-start(bf16[32,1024]{1,0:T(8,128)(2,1)S(1)} %get-tuple-element.24), channel_id=1, source_target_pairs={{0,144},{16,128},{32,176},{48,160},{64,208},{80,192},{96,240},{112... | collective-permute-start | bytes 196616 | tf_op jit(solution)/shard_map/ppermute | solution.py:61
  36.4 6.3 %collective-permute-start.10 = (bf16[32,2048]{1,0:T(8,128)(2,1)S(1)}, bf16[32,2048]{1,0:T(8,128)(2,1)S(1)}, u32[]{:S(2)}, u32[]{:S(2)}) collective-permute-start(bf16[32,2048]{1,0:T(8,128)(2,1)S(1)} %collective-permute-done.8.g2_ref), channel_id=1, source_target_pairs={{0,48},{16,224},{32,80},{48,0},{64,112},{80,32},{96,144},{112,64},... | collective-permute-start | bytes 393224 | tf_op jit(solution)/shard_map/ppermute | solution.py:61
  38.9 9.1 %collective-permute-start.9 = (bf16[32,4096]{1,0:T(8,128)(2,1)S(1)}, bf16[32,4096]{1,0:T(8,128)(2,1)S(1)}, u32[]{:S(2)}, u32[]{:S(2)}) collective-permute-start(bf16[32,4096]{1,0:T(8,128)(2,1)S(1)} %pad_maximum_fusion), channel_id=1, source_target_pairs={{0,16},{16,0},{32,48},{48,32},{64,80},{80,64},{96,112},{112,96},{1... | collective-permute-start | bytes 786440 | tf_op jit(solution)/shard_map/ppermute | solution.py:65
  42.8 6.2 %collective-permute-start.12 = (bf16[32,3072]{1,0:T(8,128)(2,1)S(1)}, bf16[32,3072]{1,0:T(8,128)(2,1)S(1)}, u32[]{:S(2)}, u32[]{:S(2)}) collective-permute-start(bf16[32,3072]{1,0:T(8,128)(2,1)S(1)} %constant_dynamic-update-slice_fusion.last_ref), channel_id=1, source_target_pairs={{0,16},{16,0},{32,48},{48,32},{64,80},{80,64},{96,112},{112,96},{1... | collective-permute-start | bytes 589832 | tf_op jit(solution)/shard_map/ppermute | solution.py:65

commit v4 on v3

--- a/solution.py
+++ b/solution.py
@@ -182,17 +182,25 @@
         sq_ref[block] = part
 
 
-def early_kernel(n_ref, g1_ref, g2_ref, w12_ref, res_out, sq_ref, sems):
+def early_kernel(n_ref, g1_ref, g2_ref, w12_ref, gain_ref, res_out, sq_ref, gained_ref, top_ref, sems):
     early, _ = pieces(*place(), n_ref, g1_ref, g2_ref, w12_ref)
     copies = write_out(early, res_out, sems)
     sq_ref[...] = jnp.zeros_like(sq_ref)
     add_squares(early, sq_ref)
+    top = jnp.zeros(top_ref.shape, f32)
+    for i, (ref, at, block) in enumerate(by_half(early)):
+        gains = gain_ref[block]
+        for j in range(0, HALF, 128):
+            x = ref[:, at + j : at + j + 128].astype(f32) * gains[:, j : j + 128]
+            top = jnp.maximum(top, jnp.abs(x))
+            gained_ref[:, i * HALF + j : i * HALF + j + 128] = x
+    top_ref[...] = top
     for copy in copies:
         copy.wait()
 
 
 def finish_kernel(
-    n_ref, g1_ref, g2_ref, w12_ref, last_ref, w34_ref, gain_ref, early_sq, _,
+    n_ref, g1_ref, g2_ref, w12_ref, last_ref, w34_ref, gain_ref, early_sq, gained_ref, top_ref, _,
     res_out, norm_out, peak_out, peak_ref, y_ref, sq_ref, res_sems, norm_sems, peak_sem,
 ):
     early, late = pieces(*place(), n_ref, g1_ref, g2_ref, w12_ref, last_ref, w34_ref)
@@ -205,13 +213,17 @@
         total += sq_ref[block]
     mean = jnp.sum(total, axis=1, keepdims=True) * (1.0 / features)
     inv = jnp.broadcast_to(lax.rsqrt(mean + 1e-05), (tokens, 128))
-    peak = jnp.zeros((tokens, 128), f32)
+    peak = top_ref[...] * inv
+    ready = len(by_half(early))
     for i, (ref, at, block) in enumerate(by_half(early + late)):
         gains = gain_ref[block]
         for j in range(0, HALF, 128):
-            x = ref[:, at + j : at + j + 128].astype(f32)
-            y = x * inv * gains[:, j : j + 128]
-            peak = jnp.maximum(peak, jnp.abs(y))
+            if i < ready:
+                y = gained_ref[:, i * HALF + j : i * HALF + j + 128] * inv
+            else:
+                x = ref[:, at + j : at + j + 128].astype(f32)
+                y = x * gains[:, j : j + 128] * inv
+                peak = jnp.maximum(peak, jnp.abs(y))
             y_ref[:, i * HALF + j : i * HALF + j + 128] = y.astype(bf16)
         copies.append(
             pltpu.make_async_copy(
@@ -342,20 +354,25 @@
     blocks = features // HALF
     gains = gain.astype(f32).reshape(blocks, 1, HALF)
     whole = jax.ShapeDtypeStruct((tokens, features), bf16)
-    begun, squares = pl.pallas_call(
+    begun, squares, gained, top = pl.pallas_call(
         early_kernel,
-        out_shape=(whole, onchip((blocks, tokens, 128), f32)),
-        in_specs=[VMEM] * 4,
-        out_specs=(ANY, VMEM),
+        out_shape=(
+            whole,
+            onchip((blocks, tokens, 128), f32),
+            onchip((tokens, 5 * CHUNK), f32),
+            onchip((tokens, 128), f32),
+        ),
+        in_specs=[VMEM] * 5,
+        out_specs=(ANY, VMEM, VMEM, VMEM),
         scratch_shapes=[dma((5,))],
         cost_estimate=cost(1_000_000, 1 << 20),
         compiler_params=SMALL,
         name="early",
-    )(*map(near, (n, g1, g2, w12)))
+    )(*map(near, (n, g1, g2, w12, gains)))
     res_out, norm_out, peak = pl.pallas_call(
         finish_kernel,
         out_shape=(whole, whole, jax.ShapeDtypeStruct((1, tokens), f32)),
-        in_specs=[VMEM] * 8 + [ANY],
+        in_specs=[VMEM] * 10 + [ANY],
         out_specs=(ANY, ANY, ANY),
         scratch_shapes=[
             pltpu.VMEM((1, tokens), f32),
@@ -365,11 +382,11 @@
             dma((blocks,)),
             dma,
         ],
-        input_output_aliases={8: 0},
+        input_output_aliases={10: 0},
         cost_estimate=cost(1_000_000, 4 << 20),
         compiler_params=SMALL,
         name="finish",
-    )(*map(near, (n, g1, g2, w12, last, w34, gains, squares)), begun)
+    )(*map(near, (n, g1, g2, w12, last, w34, gains, squares, gained, top)), begun)
     return res_out, norm_out, peak.reshape(tokens)
 
 

time: 50.6 us -> 50.6 us (level)
  no operation moved by 1% of the time
where the time goes in v4:
time: 50.6 us; the launch traced here: 50.4 us
  starting transfers between devices  23.4 us (46%)
  waiting for transfers between devices  16 us (32%)
  Pallas kernels  8.83 us (17%)
  local copies, waits for them, and re-layouts  1.35 us (3%)
  between operations  0.84 us (2%)
    ppermute x8, starting transfers between devices, along(): return lax.ppermute(x, 'tp', pairs)  16.4 us
    ppermute x8, waiting for transfers between devices, along(): return lax.ppermute(x, 'tp', pairs)  13.8 us
    ppermute x5, starting transfers between devices, across(): return lax.ppermute(x, 'tp', [(i, i ^ 1) for i in range(2 * CHIPS)])  6.93 us
    pallas_call x2, Pallas kernels, attend(): pl.pallas_call(functools.partial(attend_kernel, g * (seqs // SEQ_GROUPS))...  5.01 us
    ppermute x5, waiting for transfers between devices, across(): return lax.ppermute(x, 'tp', [(i, i ^ 1) for i in range(2 * CHIPS)])  2.24 us
    pallas_call x1, Pallas kernels, summed_and_normed(): pl.pallas_call(finish_kernel, out_shape=(whole, whole, jax.ShapeDtypeStru...  1.48 us
    pallas_call x7, Pallas kernels, call(): pl.pallas_call(kernel, out_shape=outs, in_specs=in_specs or [VMEM] * len(...  1.45 us
    unnamed x17, local copies, waits for them, and re-layouts  1.27 us
  transfers between devices with their start and end apart: 13, of which 7 were waited for; matrix products, arithmetic and copies ran while one was open for 0% of the time, Pallas kernels for 14%

profile of v4, /device:TPU:1, one launch (start us, length us, event | category | flops | bytes accessed | tf_op | source)
XLA Modules:
  0.0 50.4 jit_solution(7949641514206021870)
XLA Ops:
  0.6 1.2 %copy-done.3 = bf16[1,32,16384]{2,1,0:T(8,128)(2,1)S(1)} copy-done((bf16[1,32,16384]{2,1,0:T(8,128)(2,1)S(1)}, bf16[1,32,16384]{2,1,0:T(8,128)(2,1)}, u32[]{:S(2)}) %copy-start.3) | copy-done | bytes 1048600
  2.0 3.3 %collective-permute-start = (bf16[32,6144]{1,0:T(8,128)(2,1)S(1)}, bf16[32,6144]{1,0:T(8,128)(2,1)S(1)}, u32[]{:S(2)}, u32[]{:S(2)}) collective-permute-start(bf16[32,6144]{1,0:T(8,128)(2,1)S(1)} %shard_map.102), channel_id=1, source_target_pairs={{0,16},{16,0},{32,48},{48,32},{64,80},{80,64},{96,112},{112,96},{1... | collective-permute-start | bytes 1179656 | tf_op jit(solution)/shard_map/ppermute | solution.py:65
  5.3 1.0 %shard_map.104 = (bf16[32,2048]{1,0:T(8,128)(2,1)S(1)}, bf16[32,2048]{1,0:T(8,128)(2,1)S(1)}) custom-call(bf16[32,16384]{1,0:T(8,128)(2,1)} %bitcast.11), custom_call_target="tpu_custom_call" | custom-call | flops 4000000000 | bytes 1048576 | tf_op jit(solution)/shard_map/pallas_call | solution.py:317
  6.3 0.2 collective-permute-start.2
  6.5 1.2 %collective-permute-done.2.got_ref = bf16[32,2048]{1,0:T(8,128)(2,1)S(1)} collective-permute-done((bf16[32,2048]{1,0:T(8,128)(2,1)S(1)}, bf16[32,2048]{1,0:T(8,128)(2,1)S(1)}, u32[]{:S(2)}, u32[]{:S(2)}) %collective-permute-start.2) | collective-permute-done | bytes 131104 | tf_op jit(solution)/shard_map/ppermute | solution.py:65
  7.8 4.0 %collective-permute-start.3 = (bf16[32,2048]{1,0:T(8,128)(2,1)S(1)}, bf16[32,2048]{1,0:T(8,128)(2,1)S(1)}, u32[]{:S(2)}, u32[]{:S(2)}) collective-permute-start(bf16[32,2048]{1,0:T(8,128)(2,1)S(1)} %shard_map.105), channel_id=1, source_target_pairs={{0,48},{16,224},{32,80},{48,0},{64,112},{80,32},{96,144},{112,64},... | collective-permute-start | bytes 393224 | tf_op jit(solution)/shard_map/ppermute | solution.py:61
  11.9 2.5 %collective-permute-done.3.r3_ref = bf16[32,2048]{1,0:T(8,128)(2,1)S(1)} collective-permute-done((bf16[32,2048]{1,0:T(8,128)(2,1)S(1)}, bf16[32,2048]{1,0:T(8,128)(2,1)S(1)}, u32[]{:S(2)}, u32[]{:S(2)}) %collective-permute-start.3) | collective-permute-done | bytes 131104 | tf_op jit(solution)/shard_map/ppermute | solution.py:61
  14.6 2.1 %collective-permute-start.1 = (bf16[32,2048]{1,0:T(8,128)(2,1)S(1)}, bf16[32,2048]{1,0:T(8,128)(2,1)S(1)}, u32[]{:S(2)}, u32[]{:S(2)}) collective-permute-start(bf16[32,2048]{1,0:T(8,128)(2,1)S(1)} %get-tuple-element.19), channel_id=1, source_target_pairs={{0,32},{16,240},{32,64},{48,16},{64,96},{80,48},{96,128},{112,80},... | collective-permute-start | bytes 393224 | tf_op jit(solution)/shard_map/ppermute | solution.py:61
  16.7 4.1 %collective-permute-start.5 = (bf16[32,1024]{1,0:T(8,128)(2,1)S(1)}, bf16[32,1024]{1,0:T(8,128)(2,1)S(1)}, u32[]{:S(2)}, u32[]{:S(2)}) collective-permute-start(bf16[32,1024]{1,0:T(8,128)(2,1)S(1)} %get-tuple-element.23), channel_id=1, source_target_pairs={{0,128},{16,144},{32,160},{48,176},{64,192},{80,208},{96,224},{112... | collective-permute-start | bytes 196616 | tf_op jit(solution)/shard_map/ppermute | solution.py:61
  20.8 3.9 %collective-permute-done.5.r4_ref = bf16[32,1024]{1,0:T(8,128)(2,1)S(1)} collective-permute-done((bf16[32,1024]{1,0:T(8,128)(2,1)S(1)}, bf16[32,1024]{1,0:T(8,128)(2,1)S(1)}, u32[]{:S(2)}, u32[]{:S(2)}) %collective-permute-start.5) | collective-permute-done | bytes 65568 | tf_op jit(solution)/shard_map/ppermute | solution.py:61
  24.8 2.1 %collective-permute-start.6 = (bf16[32,2048]{1,0:T(8,128)(2,1)S(1)}, bf16[32,2048]{1,0:T(8,128)(2,1)S(1)}, u32[]{:S(2)}, u32[]{:S(2)}) collective-permute-start(bf16[32,2048]{1,0:T(8,128)(2,1)S(1)} %shard_map.107.t_ref), channel_id=1, source_target_pairs={{0,16},{16,0},{32,48},{48,32},{64,80},{80,64},{96,112},{112,96},{1... | collective-permute-start | bytes 393224 | tf_op jit(solution)/shard_map/ppermute | solution.py:65
  26.9 1.0 %collective-permute-done.6.rt_ref = bf16[32,2048]{1,0:T(8,128)(2,1)S(1)} collective-permute-done((bf16[32,2048]{1,0:T(8,128)(2,1)S(1)}, bf16[32,2048]{1,0:T(8,128)(2,1)S(1)}, u32[]{:S(2)}, u32[]{:S(2)}) %collective-permute-start.6) | collective-permute-done | bytes 131104 | tf_op jit(solution)/shard_map/ppermute | solution.py:65
  28.0 2.6 %collective-permute-start.8 = (bf16[32,2048]{1,0:T(8,128)(2,1)S(1)}, bf16[32,2048]{1,0:T(8,128)(2,1)S(1)}, u32[]{:S(2)}, u32[]{:S(2)}) collective-permute-start(bf16[32,2048]{1,0:T(8,128)(2,1)S(1)} %get-tuple-element.25.n_ref), channel_id=1, source_target_pairs={{0,208},{16,64},{32,240},{48,96},{64,16},{80,128},{96,48},{112,160... | collective-permute-start | bytes 393224 | tf_op jit(solution)/shard_map/ppermute | solution.py:61
  30.6 1.7 %collective-permute-start.7 = (bf16[32,2048]{1,0:T(8,128)(2,1)S(1)}, bf16[32,2048]{1,0:T(8,128)(2,1)S(1)}, u32[]{:S(2)}, u32[]{:S(2)}) collective-permute-start(bf16[32,2048]{1,0:T(8,128)(2,1)S(1)} %get-tuple-element.25.n_ref), channel_id=1, source_target_pairs={{0,32},{16,240},{32,64},{48,16},{64,96},{80,48},{96,128},{112,80},... | collective-permute-start | bytes 393224 | tf_op jit(solution)/shard_map/ppermute | solution.py:61
  32.3 1.6 %collective-permute-start.11 = (bf16[32,1024]{1,0:T(8,128)(2,1)S(1)}, bf16[32,1024]{1,0:T(8,128)(2,1)S(1)}, u32[]{:S(2)}, u32[]{:S(2)}) collective-permute-start(bf16[32,1024]{1,0:T(8,128)(2,1)S(1)} %get-tuple-element.26), channel_id=1, source_target_pairs={{0,144},{16,128},{32,176},{48,160},{64,208},{80,192},{96,240},{112... | collective-permute-start | bytes 196616 | tf_op jit(solution)/shard_map/ppermute | solution.py:61
  33.9 2.5 %collective-permute-done.8.g2_ref = bf16[32,2048]{1,0:T(8,128)(2,1)S(1)} collective-permute-done((bf16[32,2048]{1,0:T(8,128)(2,1)S(1)}, bf16[32,2048]{1,0:T(8,128)(2,1)S(1)}, u32[]{:S(2)}, u32[]{:S(2)}) %collective-permute-start.8) | collective-permute-done | bytes 131104 | tf_op jit(solution)/shard_map/ppermute | solution.py:61
  36.4 0.2 collective-permute-start.10
  36.6 2.3 %collective-permute-done.7.g1_ref = bf16[32,2048]{1,0:T(8,128)(2,1)S(1)} collective-permute-done((bf16[32,2048]{1,0:T(8,128)(2,1)S(1)}, bf16[32,2048]{1,0:T(8,128)(2,1)S(1)}, u32[]{:S(2)}, u32[]{:S(2)}) %collective-permute-start.7) | collective-permute-done | bytes 131104 | tf_op jit(solution)/shard_map/ppermute | solution.py:61
  38.9 1.2 %collective-permute-start.9 = (bf16[32,4096]{1,0:T(8,128)(2,1)S(1)}, bf16[32,4096]{1,0:T(8,128)(2,1)S(1)}, u32[]{:S(2)}, u32[]{:S(2)}) collective-permute-start(bf16[32,4096]{1,0:T(8,128)(2,1)S(1)} %pad_maximum_fusion), channel_id=1, source_target_pairs={{0,16},{16,0},{32,48},{48,32},{64,80},{80,64},{96,112},{112,96},{1... | collective-permute-start | bytes 786440 | tf_op jit(solution)/shard_map/ppermute | solution.py:65
  40.2 2.6 %collective-permute-done.10 = bf16[32,2048]{1,0:T(8,128)(2,1)S(1)} collective-permute-done((bf16[32,2048]{1,0:T(8,128)(2,1)S(1)}, bf16[32,2048]{1,0:T(8,128)(2,1)S(1)}, u32[]{:S(2)}, u32[]{:S(2)}) %collective-permute-start.10) | collective-permute-done | bytes 131104 | tf_op jit(solution)/shard_map/ppermute | solution.py:61
  43.0 2.5 %shard_map.109.refs_0_ = bf16[32,1024]{1,0:T(8,128)(2,1)} custom-call(bf16[32,1024]{1,0:T(8,128)(2,1)S(1)} %copy-done.2, bf16[32,512,128]{2,1,0:T(8,128)(2,1)S(1)} %bitcast.5, bf16[32,512,128]{2,1,0:T(8,128)(2,1)S(1)} %bitcast.7, s32[32,128]{1,0:T(8,128)S(1)} %broadcast_in_dim.2.len_ref), custom_call_target="tpu_custom_call" | custom-call | flops 200000000 | bytes 4194304 | tf_op jit(solution)/shard_map/pallas_call | solution.py:289
  45.5 2.5 %shard_map.110 = bf16[32,1024]{1,0:T(8,128)(2,1)} custom-call(bf16[32,1024]{1,0:T(8,128)(2,1)S(1)} %copy-done.2, bf16[32,512,128]{2,1,0:T(8,128)(2,1)S(1)} %bitcast.6, bf16[32,512,128]{2,1,0:T(8,128)(2,1)S(1)} %bitcast.8, s32[32,128]{1,0:T(8,128)S(1)} %broadcast_in_dim.2.len_ref, bf16[32,1024]{1,0:T(8,128)(2,1)} %shard_map.109.refs_0_), custom_call_target="tpu_custom_call", output_to_operand_aliasing={{}: (4, {})} | custom-call | flops 200000000 | bytes 4194304 | tf_op jit(solution)/shard_map/pallas_call | solution.py:289
  48.0 0.9 %early.1 = (bf16[32,16384]{1,0:T(8,128)(2,1)}, f32[16,32,128]{2,1,0:T(8,128)S(1)}, f32[32,10240]{1,0:T(8,128)S(1)}, f32[32,128]{1,0:T(8,128)S(1)}) custom-call(bf16[32,2048]{1,0:T(8,128)(2,1)S(1)} %get-tuple-element.25.n_ref, bf16[32,2048]{1,0:T(8,128)(2,1)S(1)} %collective-permute-done.7.g1_ref, bf16[32,2048]{1,0:T(8,128)(2,1)S(1)} %collective-permute-done.8.g2_ref, ...), custom_call_target="tpu_custom_call" | custom-call | flops 1000000 | bytes 1048576 | tf_op jit(solution)/shard_map/early/pallas_call | solution.py:357
  48.9 1.5 %finish.1 = (bf16[32,16384]{1,0:T(8,128)(2,1)}, bf16[32,16384]{1,0:T(8,128)(2,1)}, f32[1,32]{1,0:T(1,128)}) custom-call(bf16[32,2048]{1,0:T(8,128)(2,1)S(1)} %get-tuple-element.25.n_ref, bf16[32,2048]{1,0:T(8,128)(2,1)S(1)} %collective-permute-done.7.g1_ref, bf16[32,2048]{1,0:T(8,128)(2,1)S(1)} %collective-permute-done.8.g2_ref, ...), custom_call_target="tpu_custom_call", output_to_operand_aliasing={{0}: (10, {})} | custom-call | flops 1000000 | bytes 4194304 | tf_op jit(solution)/shard_map/finish/pallas_call | solution.py:372
  (34 shorter events, 0.8 us)
Async XLA Ops:
  0.6 1.2 %copy-start.3 = (bf16[1,32,16384]{2,1,0:T(8,128)(2,1)S(1)}, bf16[1,32,16384]{2,1,0:T(8,128)(2,1)}, u32[]{:S(2)}) copy-start(bf16[1,32,16384]{2,1,0:T(8,128)(2,1)} %param.7) | copy-start | bytes 3145732
  2.0 9.8 %copy-start.4 = (bf16[1,32,16384]{2,1,0:T(8,128)(2,1)S(1)}, bf16[1,32,16384]{2,1,0:T(8,128)(2,1)}, u32[]{:S(2)}) copy-start(bf16[1,32,16384]{2,1,0:T(8,128)(2,1)} %param.7) | copy-start | bytes 3145732
  2.0 9.7 %collective-permute-start = (bf16[32,6144]{1,0:T(8,128)(2,1)S(1)}, bf16[32,6144]{1,0:T(8,128)(2,1)S(1)}, u32[]{:S(2)}, u32[]{:S(2)}) collective-permute-start(bf16[32,6144]{1,0:T(8,128)(2,1)S(1)} %shard_map.102), channel_id=1, source_target_pairs={{0,16},{16,0},{32,48},{48,32},{64,80},{80,64},{96,112},{112,96},{1... | collective-permute-start | bytes 1179656 | tf_op jit(solution)/shard_map/ppermute | solution.py:65
  6.3 1.4 %collective-permute-start.2 = (bf16[32,2048]{1,0:T(8,128)(2,1)S(1)}, bf16[32,2048]{1,0:T(8,128)(2,1)S(1)}, u32[]{:S(2)}, u32[]{:S(2)}) collective-permute-start(bf16[32,2048]{1,0:T(8,128)(2,1)S(1)} %get-tuple-element.22), channel_id=1, source_target_pairs={{0,16},{16,0},{32,48},{48,32},{64,80},{80,64},{96,112},{112,96},{1... | collective-permute-start | bytes 393224 | tf_op jit(solution)/shard_map/ppermute | solution.py:65
  7.8 6.6 %collective-permute-start.3 = (bf16[32,2048]{1,0:T(8,128)(2,1)S(1)}, bf16[32,2048]{1,0:T(8,128)(2,1)S(1)}, u32[]{:S(2)}, u32[]{:S(2)}) collective-permute-start(bf16[32,2048]{1,0:T(8,128)(2,1)S(1)} %shard_map.105), channel_id=1, source_target_pairs={{0,48},{16,224},{32,80},{48,0},{64,112},{80,32},{96,144},{112,64},... | collective-permute-start | bytes 393224 | tf_op jit(solution)/shard_map/ppermute | solution.py:61
  11.9 16.0 %copy-start.5 = (bf16[32,16384]{1,0:T(8,128)(2,1)S(1)}, bf16[32,16384]{1,0:T(8,128)(2,1)}, u32[]{:S(2)}) copy-start(bf16[32,16384]{1,0:T(8,128)(2,1)} %res_ref.1) | copy-start | bytes 3145732
  14.4 28.6 %copy-start.2 = (bf16[32,1024]{1,0:T(8,128)(2,1)S(1)}, bf16[32,1024]{1,0:T(8,128)(2,1)}, u32[]{:S(2)}) copy-start(bf16[32,1024]{1,0:T(8,128)(2,1)} %q_ref.3) | copy-start | bytes 196612
  14.5 28.4 %copy-start.6 = (bf16[16384]{0:T(1024)(128)(2,1)S(1)}, bf16[16384]{0:T(1024)(128)(2,1)}, u32[]{:S(2)}) copy-start(bf16[16384]{0:T(1024)(128)(2,1)} %param.9) | copy-start | bytes 98308
  14.5 10.2 %collective-permute-start.4 = (bf16[32,2048]{1,0:T(8,128)(2,1)S(1)}, bf16[32,2048]{1,0:T(8,128)(2,1)S(1)}, u32[]{:S(2)}, u32[]{:S(2)}) collective-permute-start(bf16[32,2048]{1,0:T(8,128)(2,1)S(1)} %shard_map.106), channel_id=1, source_target_pairs={{0,208},{16,64},{32,240},{48,96},{64,16},{80,128},{96,48},{112,160... | collective-permute-start | bytes 393224 | tf_op jit(solution)/shard_map/ppermute | solution.py:61
  14.6 10.1 %collective-permute-start.1 = (bf16[32,2048]{1,0:T(8,128)(2,1)S(1)}, bf16[32,2048]{1,0:T(8,128)(2,1)S(1)}, u32[]{:S(2)}, u32[]{:S(2)}) collective-permute-start(bf16[32,2048]{1,0:T(8,128)(2,1)S(1)} %get-tuple-element.19), channel_id=1, source_target_pairs={{0,32},{16,240},{32,64},{48,16},{64,96},{80,48},{96,128},{112,80},... | collective-permute-start | bytes 393224 | tf_op jit(solution)/shard_map/ppermute | solution.py:61
  16.7 8.0 %collective-permute-start.5 = (bf16[32,1024]{1,0:T(8,128)(2,1)S(1)}, bf16[32,1024]{1,0:T(8,128)(2,1)S(1)}, u32[]{:S(2)}, u32[]{:S(2)}) collective-permute-start(bf16[32,1024]{1,0:T(8,128)(2,1)S(1)} %get-tuple-element.23), channel_id=1, source_target_pairs={{0,128},{16,144},{32,160},{48,176},{64,192},{80,208},{96,224},{112... | collective-permute-start | bytes 196616 | tf_op jit(solution)/shard_map/ppermute | solution.py:61
  24.7 18.2 %copy-start.7 = (s32[32]{0:T(128)S(1)}, s32[32]{0:T(128)}, u32[]{:S(2)}) copy-start(s32[32]{0:T(128)} %param.13) | copy-start | bytes 388
  24.7 18.3 %copy-start = (bf16[1,32,512,128]{3,2,1,0:T(8,128)(2,1)S(1)}, bf16[1,32,512,128]{3,2,1,0:T(8,128)(2,1)}, u32[]{:S(2)}) copy-start(bf16[1,32,512,128]{3,2,1,0:T(8,128)(2,1)} %param.11) | copy-start | bytes 12582916
  24.7 18.3 %copy-start.1 = (bf16[1,32,512,128]{3,2,1,0:T(8,128)(2,1)S(1)}, bf16[1,32,512,128]{3,2,1,0:T(8,128)(2,1)}, u32[]{:S(2)}) copy-start(bf16[1,32,512,128]{3,2,1,0:T(8,128)(2,1)} %param.12) | copy-start | bytes 12582916
  24.8 3.1 %collective-permute-start.6 = (bf16[32,2048]{1,0:T(8,128)(2,1)S(1)}, bf16[32,2048]{1,0:T(8,128)(2,1)S(1)}, u32[]{:S(2)}, u32[]{:S(2)}) collective-permute-start(bf16[32,2048]{1,0:T(8,128)(2,1)S(1)} %shard_map.107.t_ref), channel_id=1, source_target_pairs={{0,16},{16,0},{32,48},{48,32},{64,80},{80,64},{96,112},{112,96},{1... | collective-permute-start | bytes 393224 | tf_op jit(solution)/shard_map/ppermute | solution.py:65
  28.0 8.4 %collective-permute-start.8 = (bf16[32,2048]{1,0:T(8,128)(2,1)S(1)}, bf16[32,2048]{1,0:T(8,128)(2,1)S(1)}, u32[]{:S(2)}, u32[]{:S(2)}) collective-permute-start(bf16[32,2048]{1,0:T(8,128)(2,1)S(1)} %get-tuple-element.25.n_ref), channel_id=1, source_target_pairs={{0,208},{16,64},{32,240},{48,96},{64,16},{80,128},{96,48},{112,160... | collective-permute-start | bytes 393224 | tf_op jit(solution)/shard_map/ppermute | solution.py:61
  30.6 8.3 %collective-permute-start.7 = (bf16[32,2048]{1,0:T(8,128)(2,1)S(1)}, bf16[32,2048]{1,0:T(8,128)(2,1)S(1)}, u32[]{:S(2)}, u32[]{:S(2)}) collective-permute-start(bf16[32,2048]{1,0:T(8,128)(2,1)S(1)} %get-tuple-element.25.n_ref), channel_id=1, source_target_pairs={{0,32},{16,240},{32,64},{48,16},{64,96},{80,48},{96,128},{112,80},... | collective-permute-start | bytes 393224 | tf_op jit(solution)/shard_map/ppermute | solution.py:61
  32.3 10.5 %collective-permute-start.11 = (bf16[32,1024]{1,0:T(8,128)(2,1)S(1)}, bf16[32,1024]{1,0:T(8,128)(2,1)S(1)}, u32[]{:S(2)}, u32[]{:S(2)}) collective-permute-start(bf16[32,1024]{1,0:T(8,128)(2,1)S(1)} %get-tuple-element.26), channel_id=1, source_target_pairs={{0,144},{16,128},{32,176},{48,160},{64,208},{80,192},{96,240},{112... | collective-permute-start | bytes 196616 | tf_op jit(solution)/shard_map/ppermute | solution.py:61
  36.4 6.3 %collective-permute-start.10 = (bf16[32,2048]{1,0:T(8,128)(2,1)S(1)}, bf16[32,2048]{1,0:T(8,128)(2,1)S(1)}, u32[]{:S(2)}, u32[]{:S(2)}) collective-permute-start(bf16[32,2048]{1,0:T(8,128)(2,1)S(1)} %collective-permute-done.8.g2_ref), channel_id=1, source_target_pairs={{0,48},{16,224},{32,80},{48,0},{64,112},{80,32},{96,144},{112,64},... | collective-permute-start | bytes 393224 | tf_op jit(solution)/shard_map/ppermute | solution.py:61
  38.9 9.1 %collective-permute-start.9 = (bf16[32,4096]{1,0:T(8,128)(2,1)S(1)}, bf16[32,4096]{1,0:T(8,128)(2,1)S(1)}, u32[]{:S(2)}, u32[]{:S(2)}) collective-permute-start(bf16[32,4096]{1,0:T(8,128)(2,1)S(1)} %pad_maximum_fusion), channel_id=1, source_target_pairs={{0,16},{16,0},{32,48},{48,32},{64,80},{80,64},{96,112},{112,96},{1... | collective-permute-start | bytes 786440 | tf_op jit(solution)/shard_map/ppermute | solution.py:65
  42.8 6.2 %collective-permute-start.12 = (bf16[32,3072]{1,0:T(8,128)(2,1)S(1)}, bf16[32,3072]{1,0:T(8,128)(2,1)S(1)}, u32[]{:S(2)}, u32[]{:S(2)}) collective-permute-start(bf16[32,3072]{1,0:T(8,128)(2,1)S(1)} %constant_dynamic-update-slice_fusion.last_ref), channel_id=1, source_target_pairs={{0,16},{16,0},{32,48},{48,32},{64,80},{80,64},{96,112},{112,96},{1... | collective-permute-start | bytes 589832 | tf_op jit(solution)/shard_map/ppermute | solution.py:65
